TPU v7x, 512 devices: a whole 4x8x8 slice. The times are simulated.
512 devices in a mesh: coil: 32 (over x, z), frame: 16 (over y, core).
Axes of the slice: x: 4, y: 8, z: 8, core: 2. Of those that a mesh axis runs over, the one named last changes fastest.
Arguments:
- initial_image: float32 [256, 16, 2, 256], P('coil', 'frame'), may hold values from -3 to 3
- coil_maps: bfloat16 [32, 2, 256, 256], P('coil'), may hold values from -1.5 to 1.5
- samples: bfloat16 [32, 16, 18, 2, 256], P('coil', 'frame'), may hold values from -6 to 6
- blocks_used: int32 [16], P('frame'), may hold values from 1 to 18, 145 in all
- row_offset: int32 [16, 18], P('frame'), may hold values from 0 to 128
- col_offset: int32 [16, 18], P('frame'), may hold values from 0 to 128
- row_first: int32 [16, 18, 256], P('frame'), may hold values from 0 to 124
- col_first: int32 [16, 18, 256], P('frame'), may hold values from 0 to 124
- row_taps: bfloat16 [16, 18, 4, 256], P('frame'), may hold values from 0.099609375 to 0.59765625
- col_taps: bfloat16 [16, 18, 4, 256], P('frame'), may hold values from 0.099609375 to 0.59765625
Outputs:
- image: float32 [256, 16, 2, 256], P('coil', 'frame')
- misfit: float32 [2, 16], P(None, 'frame')
Inputs may be any that keep to these rules, and one draw needn't show every extreme that they name: Blocks 0 to blocks_used minus one of the frame were acquired. `row_first`: the kernel's 4 rows lie inside the tile. `col_first`: the kernel's 4 columns lie inside the tile.
All inputs are finite; a program needn't handle non-finite values.
Results may differ from a plain program's by a relative error of at most 0.006.
Values may be sent and summed in bfloat16 or wider, within the bound.
No kernel may reach another device: no remote copies, remote signals or barrier semaphores. Data moves between devices by JAX's collectives and lax.ppermute only.
A program may use at most 64 MiB of HBM per device.

v0:
```python
import math

import jax
import jax.numpy as jnp
from jax import lax
from jax.sharding import PartitionSpec as P

N = 256
NB = 18
BS = 256
TT = 128
KW = 4
ITERS = 2


step_size = 2.0
tv_weight = 0.1
smooth_floor = 0.5
shrink_weight = 0.1


def laid_out(parts, dim):
    parts = jnp.moveaxis(parts, 0, dim)
    lengths = parts.shape
    return parts.reshape(*lengths[:dim], lengths[dim] * lengths[dim + 1], *lengths[dim + 2 :])


def sent_to_all(array, axis):
    copies = jnp.broadcast_to(array, (lax.axis_size(axis), *array.shape))
    return lax.all_to_all(copies, axis, split_axis=0, concat_axis=0, tiled=True)


def gather_directly(array, axis, dim):
    return laid_out(sent_to_all(array, axis), dim)


def split_up(array, dim, length):
    before, after = (array.shape[:dim], array.shape[dim + 1 :])
    return jnp.moveaxis(array.reshape(*before, length, -1, *after), dim, 0)


def summed_on_arrival(array, axis, dim):
    length = lax.axis_size(axis)
    parts = lax.all_to_all(split_up(array, dim, length), axis, 0, 0, tiled=True)
    return jnp.sum(parts, axis=0)


def extended(cells, sides, width):
    for axis, dim in sides:
        count = lax.axis_size(axis)
        head = lax.slice_in_dim(cells, 0, width, axis=dim)
        tail = lax.slice_in_dim(cells, cells.shape[dim] - width, cells.shape[dim], axis=dim)
        cells = jnp.concatenate(
            [
                lax.ppermute(tail, axis, [(i, (i + 1) % count) for i in range(count)]),
                cells,
                lax.ppermute(head, axis, [((i + 1) % count, i) for i in range(count)]),
            ],
            axis=dim,
        )
    return cells


def taken_together(array, axis):
    everything = sent_to_all(array, axis)
    return jnp.sum(everything, axis=0)


def rounded(values):
    return lax.optimization_barrier(values.astype(jnp.bfloat16))


def pair_tables(order):
    counter = jnp.arange(order, dtype=jnp.int32)
    phase = counter[:, None] * counter[None, :] % order
    angle = phase.astype(jnp.float32) * (2.0 * math.pi / order)
    cosine = (jnp.cos(angle) / math.sqrt(order)).astype(jnp.bfloat16)
    sine = (jnp.sin(angle) / math.sqrt(order)).astype(jnp.bfloat16)
    table_one = jnp.stack([jnp.stack([cosine, sine]), jnp.stack([-sine, cosine])])
    table_two = jnp.stack([jnp.stack([cosine, -sine]), jnp.stack([sine, cosine])])
    return (table_one, table_two)


def tap_matrix(first_idx, taps):
    positions = jnp.arange(TT, dtype=jnp.int32)
    matrix = jnp.zeros((first_idx.shape[0], TT), jnp.float32)
    for offset in range(KW):
        hits = positions[None, :] == first_idx[:, None] + offset
        matrix = matrix + jnp.where(hits, taps[offset].astype(jnp.float32)[:, None], 0.0)
    return matrix.astype(jnp.bfloat16)


def spoke_block(
    kspace, grid_sum, tile_row, tile_col, first_row, first_col, taps_row, taps_col, measured
):
    rows_matrix = tap_matrix(first_row, taps_row)
    cols_matrix = tap_matrix(first_col, taps_col)
    anchor = jnp.zeros((), jnp.int32)
    corner = (anchor, tile_row, tile_col)
    grid_tile = lax.dynamic_slice(kspace, corner, (2, TT, TT))
    across = jnp.einsum("si,pij->psj", rows_matrix, grid_tile, preferred_element_type=jnp.float32)
    cols_wide = cols_matrix.astype(jnp.float32)
    predicted = jnp.sum(across * cols_wide[None], axis=2)
    resid = predicted - measured.astype(jnp.float32)
    misfit = jnp.sum(resid * resid)
    resid_low = rounded(resid)
    weighted = (resid_low.astype(jnp.float32)[:, :, None] * cols_wide[None]).astype(jnp.bfloat16)
    spread = jnp.einsum("si,psj->pij", rows_matrix, weighted, preferred_element_type=jnp.float32)
    updated = lax.dynamic_slice(grid_sum, corner, (2, TT, TT)) + spread
    return (lax.dynamic_update_slice(grid_sum, updated, corner), misfit)


def cine_gradient(padded):
    change = padded[:, 1:] - padded[:, :-1]
    length = jnp.sqrt(jnp.sum(change * change, axis=2, keepdims=True) + smooth_floor * smooth_floor)
    normed = change / length
    return normed[:, :-1] - normed[:, 1:]


def shrink(detail, limit):
    length = jnp.sqrt(jnp.sum(detail * detail, axis=2, keepdims=True))
    return detail * (jnp.maximum(length - limit, 0.0) / jnp.maximum(length, limit))


def wavelet_prox(field, limit):
    even_rows = field[0::2]
    odd_rows = field[1::2]
    top_left = even_rows[..., 0::2]
    top_right = even_rows[..., 1::2]
    low_left = odd_rows[..., 0::2]
    low_right = odd_rows[..., 1::2]
    approx = (top_left + top_right + low_left + low_right) * 0.5
    horiz = shrink((top_left - top_right + low_left - low_right) * 0.5, limit)
    vertical = shrink((top_left + top_right - low_left - low_right) * 0.5, limit)
    diagonal = shrink((top_left - top_right - low_left + low_right) * 0.5, limit)
    new_tl = (approx + horiz + vertical + diagonal) * 0.5
    new_tr = (approx - horiz + vertical - diagonal) * 0.5
    new_ll = (approx + horiz - vertical - diagonal) * 0.5
    new_lr = (approx - horiz - vertical + diagonal) * 0.5
    top_rows = jnp.stack([new_tl, new_tr], axis=-1).reshape(even_rows.shape)
    low_rows = jnp.stack([new_ll, new_lr], axis=-1).reshape(odd_rows.shape)
    return jnp.stack([top_rows, low_rows], axis=1).reshape(field.shape)


def on_device(
    initial_image,
    coil_maps,
    samples,
    blocks_used,
    row_offset,
    col_offset,
    row_first,
    col_first,
    row_taps,
    col_taps,
):
    table_one, table_two = pair_tables(N)
    coil_count = coil_maps.shape[0]
    image_size = coil_maps.shape[3]
    misfit_scale = 0.5 / (coil_count * lax.axis_size("coil") * NB * BS)
    current = initial_image
    moving = current
    momentum = 1.0
    misfit_rows = []
    for step_num in range(ITERS):
        image_low = rounded(moving)
        maps_wide = coil_maps.astype(jnp.float32)
        image_wide = gather_directly(image_low, "coil", 0).astype(jnp.float32)
        real_part = (
            maps_wide[:, 0][:, :, None, :] * image_wide[None, :, :, 0]
            - maps_wide[:, 1][:, :, None, :] * image_wide[None, :, :, 1]
        )
        imag_part = (
            maps_wide[:, 0][:, :, None, :] * image_wide[None, :, :, 1]
            + maps_wide[:, 1][:, :, None, :] * image_wide[None, :, :, 0]
        )
        coil_image = jnp.stack([real_part, imag_part], axis=3).astype(jnp.bfloat16)
        half_sum = jnp.einsum(
            "qprk,ckfpn->cfqrn", table_one, coil_image, preferred_element_type=jnp.float32
        )
        half_low = half_sum.astype(jnp.bfloat16)
        kspace = jnp.einsum(
            "cfprk,pqkn->cfqrn", half_low, table_two, preferred_element_type=jnp.float32
        ).astype(jnp.bfloat16)
        kspace_frame = kspace[0, 0]

        def visit(block_id, running):
            grid_sum, misfit_sum = running
            tile_row = lax.dynamic_index_in_dim(row_offset[0], block_id, 0, keepdims=False)
            tile_col = lax.dynamic_index_in_dim(col_offset[0], block_id, 0, keepdims=False)
            first_row = lax.dynamic_index_in_dim(row_first[0], block_id, 0, keepdims=False)
            first_col = lax.dynamic_index_in_dim(col_first[0], block_id, 0, keepdims=False)
            taps_row = lax.dynamic_index_in_dim(row_taps[0], block_id, 0, keepdims=False)
            taps_col = lax.dynamic_index_in_dim(col_taps[0], block_id, 0, keepdims=False)
            measured = lax.dynamic_index_in_dim(samples[0, 0], block_id, 0, keepdims=False)
            grid_sum, misfit = spoke_block(
                kspace_frame,
                grid_sum,
                tile_row,
                tile_col,
                first_row,
                first_col,
                taps_row,
                taps_col,
                measured,
            )
            return (grid_sum, misfit_sum + misfit)

        initial = (jnp.zeros((2, image_size, image_size), jnp.float32), jnp.zeros((), jnp.float32))
        grid_sum, misfit = lax.fori_loop(0, blocks_used[0], visit, initial)
        frame_grids = [grid_sum]
        frame_misfits = [misfit]
        coil_grids = [jnp.stack(frame_grids)]
        misfit_coils = [jnp.stack(frame_misfits)]
        grid_low = jnp.stack(coil_grids).astype(jnp.bfloat16)
        misfit_local = jnp.sum(jnp.stack(misfit_coils), axis=0)
        back_half = jnp.einsum(
            "qprk,cfpkn->cfqrn", table_two, grid_low, preferred_element_type=jnp.float32
        ).astype(jnp.bfloat16)
        adjoint_maps_wide = coil_maps.astype(jnp.float32)
        coil_back = jnp.einsum(
            "cfprk,pqkn->crfqn", back_half, table_one, preferred_element_type=jnp.float32
        )
        adjoint_real_part = (
            adjoint_maps_wide[:, 0][:, :, None, :] * coil_back[:, :, :, 0]
            + adjoint_maps_wide[:, 1][:, :, None, :] * coil_back[:, :, :, 1]
        )
        adjoint_imag_part = (
            adjoint_maps_wide[:, 0][:, :, None, :] * coil_back[:, :, :, 1]
            - adjoint_maps_wide[:, 1][:, :, None, :] * coil_back[:, :, :, 0]
        )
        data_grad = summed_on_arrival(
            jnp.sum(jnp.stack([adjoint_real_part, adjoint_imag_part], axis=3), axis=0), "coil", 0
        )
        misfit_rows.append(misfit_local)
        padded = extended(moving, (("frame", 1),), 1)
        descent = moving - step_size * (data_grad + tv_weight * cine_gradient(padded))
        updated = wavelet_prox(descent, step_size * shrink_weight)
        following = (1.0 + math.sqrt(1.0 + 4.0 * momentum * momentum)) / 2.0
        moving = updated + (momentum - 1.0) / following * (updated - current)
        current = updated
        momentum = following
    misfit_out = taken_together(jnp.stack(misfit_rows), "coil") * misfit_scale
    return (current, misfit_out)


def solution(mesh):
    placed = (
        P("coil", "frame", None, None),
        P("coil", None, None, None),
        P("coil", "frame", None, None, None),
        P("frame"),
        P("frame", None),
        P("frame", None),
        P("frame", None, None),
        P("frame", None, None),
        P("frame", None, None, None),
        P("frame", None, None, None),
    )
    return jax.shard_map(
        on_device,
        mesh=mesh,
        in_specs=placed,
        out_specs=(P("coil", "frame", None, None), P(None, "frame")),
        check_vma=False,
    )
```

profile of v0, /device:TPU:1, one launch (start us, length us, event | category | flops | bytes accessed | tf_op | source)
XLA Modules:
  0.0 544.8 jit_solution(14785067874741562425)
XLA Ops:
  2.1 13.8 %all-to-all-start = ((bf16[32,8,1,2,256]{4,1,3,2,0:T(8,128)(2,1)}), bf16[32,8,1,2,256]{4,1,3,2,0:T(8,128)(2,1)S(1)}, u32[]{:S(2)}, u32[]{:S(2)}) async-start(bf16[32,8,1,2,256]{4,1,3,2,0:T(8,128)(2,1)} %broadcast_in_dim.177), calls=%async_computation | async-start | bytes 524288 | tf_op jit(solution)/shard_map/all_to_all | solution.py:30
  18.3 7.3 %all-to-all-done = bf16[32,8,1,2,256]{4,1,3,2,0:T(8,128)(2,1)S(1)} async-done(((bf16[32,8,1,2,256]{4,1,3,2,0:T(8,128)(2,1)}), bf16[32,8,1,2,256]{4,1,3,2,0:T(8,128)(2,1)S(1)}, u32[]{:S(2)}, u32[]{:S(2)}) %all-to-all-start) | async-done | bytes 262176 | tf_op jit(solution)/shard_map/all_to_all | solution.py:30
  27.3 223.9 %while.24 = (s32[]{:T(128)}, f32[2,256,256]{1,2,0:T(8,128)S(1)}, f32[]{:T(128)}, s32[]{:T(128)}, s32[1,18]{1,0:T(1,128)S(1)}, /*index=5*/s32[1,18]{1,0:T(1,128)S...) while((s32[]{:T(128)}, f32[2,256,256]{1,2,0:T(8,128)S(1)}, ...), condition=%wide.region_3.4_spmd, body=%wide.region_0.3_spmd.sunk | while | flops 35067916 | bytes 1305991 | solution.py:210
  36.8 2.2 dynamic_update_slice.8
  60.7 2.3 dynamic_update_slice.8
  73.1 2.5 dynamic_update_slice.8
  85.7 2.2 dynamic_update_slice.8
  98.1 2.3 dynamic_update_slice.8
  110.5 2.4 dynamic_update_slice.8
  123.0 2.2 dynamic_update_slice.8
  135.4 2.3 dynamic_update_slice.8
  147.8 2.4 dynamic_update_slice.8
  160.4 2.2 dynamic_update_slice.8
  172.7 2.4 dynamic_update_slice.8
  185.3 2.4 dynamic_update_slice.8
  197.8 2.4 dynamic_update_slice.8
  210.4 2.4 dynamic_update_slice.8
  222.9 2.4 dynamic_update_slice.8
  235.4 2.1 dynamic_update_slice.8
  247.7 2.2 dynamic_update_slice.8
  253.1 6.5 %all-to-all-start.1 = ((f32[32,8,1,2,256]{4,1,3,2,0:T(8,128)}), f32[32,8,1,2,256]{4,1,3,2,0:T(8,128)S(1)}, u32[]{:S(2)}, u32[]{:S(2)}) async-start(f32[32,8,1,2,256]{4,1,3,2,0:T(8,128)} %copy.178), calls=%async_computation.1 | async-start | bytes 1048576 | tf_op jit(solution)/shard_map/all_to_all | solution.py:44
  259.7 1.7 collective-permute-start.1
  262.9 8.1 %all-to-all-done.1 = f32[32,8,1,2,256]{4,1,3,2,0:T(8,128)S(1)} async-done(((f32[32,8,1,2,256]{4,1,3,2,0:T(8,128)}), f32[32,8,1,2,256]{4,1,3,2,0:T(8,128)S(1)}, u32[]{:S(2)}, u32[]{:S(2)}) %all-to-all-start.1) | async-done | bytes 524320 | tf_op jit(solution)/shard_map/all_to_all | solution.py:44
  273.5 5.5 %all-to-all-start.2 = ((bf16[32,8,1,2,256]{4,1,3,2,0:T(8,128)(2,1)}), bf16[32,8,1,2,256]{4,1,3,2,0:T(8,128)(2,1)S(1)}, u32[]{:S(2)}, u32[]{:S(2)}) async-start(bf16[32,8,1,2,256]{4,1,3,2,0:T(8,128)(2,1)} %broadcast_in_dim.178), calls=%async_computation.2 | async-start | bytes 524288 | tf_op jit(solution)/shard_map/all_to_all | solution.py:30
  278.9 9.6 %all-to-all-done.2 = bf16[32,8,1,2,256]{4,1,3,2,0:T(8,128)(2,1)S(1)} async-done(((bf16[32,8,1,2,256]{4,1,3,2,0:T(8,128)(2,1)}), bf16[32,8,1,2,256]{4,1,3,2,0:T(8,128)(2,1)S(1)}, u32[]{:S(2)}, u32[]{:S(2)}) %all-to-all-start.2) | async-done | bytes 262176 | tf_op jit(solution)/shard_map/all_to_all | solution.py:30
  289.7 223.8 %while.25 = (s32[]{:T(128)}, f32[2,256,256]{1,2,0:T(8,128)S(1)}, f32[]{:T(128)}, s32[]{:T(128)}, s32[1,18]{1,0:T(1,128)S(1)}, /*index=5*/s32[1,18]{1,0:T(1,128)S...) while((s32[]{:T(128)}, f32[2,256,256]{1,2,0:T(8,128)S(1)}, ...), condition=%wide.region_12.13_spmd, body=%wide.region_9.12_spmd.sunk | while | flops 35067916 | bytes 1305991 | solution.py:210
  299.2 2.2 dynamic_update_slice.9
  323.0 2.3 dynamic_update_slice.9
  335.4 2.5 dynamic_update_slice.9
  348.0 2.2 dynamic_update_slice.9
  360.4 2.3 dynamic_update_slice.9
  372.8 2.4 dynamic_update_slice.9
  385.4 2.2 dynamic_update_slice.9
  397.7 2.3 dynamic_update_slice.9
  410.2 2.4 dynamic_update_slice.9
  422.7 2.2 dynamic_update_slice.9
  435.0 2.4 dynamic_update_slice.9
  447.6 2.4 dynamic_update_slice.9
  460.1 2.4 dynamic_update_slice.9
  472.7 2.4 dynamic_update_slice.9
  485.2 2.4 dynamic_update_slice.9
  497.7 2.1 dynamic_update_slice.9
  510.0 2.2 dynamic_update_slice.9
  514.2 4.6 all-to-all-start.4
  520.6 6.6 %all-to-all-done.4 = f32[32,2,1]{1,2,0:T(1,128)S(1)} async-done(((f32[32,2,1]{1,2,0:T(1,128)}), f32[32,2,1]{1,2,0:T(1,128)S(1)}, u32[]{:S(2)}, u32[]{:S(2)}) %all-to-all-start.4) | async-done | bytes 288 | tf_op jit(solution)/shard_map/all_to_all | solution.py:30
  527.2 3.9 all-to-all-start.3
  531.1 1.7 collective-permute-start.3
  534.9 7.6 %all-to-all-done.3 = f32[32,8,1,2,256]{4,1,3,2,0:T(8,128)S(1)} async-done(((f32[32,8,1,2,256]{4,1,3,2,0:T(8,128)}), f32[32,8,1,2,256]{4,1,3,2,0:T(8,128)S(1)}, u32[]{:S(2)}, u32[]{:S(2)}) %all-to-all-start.3) | async-done | bytes 524320 | tf_op jit(solution)/shard_map/all_to_all | solution.py:44
  (499 shorter events, 203.9 us)
Async XLA Ops:
  2.1 13.8 %copy-start.1 = (bf16[1,2,256,256]{3,2,1,0:T(8,128)(2,1)S(1)}, bf16[1,2,256,256]{3,2,1,0:T(8,128)(2,1)}, u32[]{:S(2)}) copy-start(bf16[1,2,256,256]{3,2,1,0:T(8,128)(2,1)} %param.15) | copy-start | bytes 786436
  2.1 23.5 %all-to-all-start = ((bf16[32,8,1,2,256]{4,1,3,2,0:T(8,128)(2,1)}), bf16[32,8,1,2,256]{4,1,3,2,0:T(8,128)(2,1)S(1)}, u32[]{:S(2)}, u32[]{:S(2)}) async-start(bf16[32,8,1,2,256]{4,1,3,2,0:T(8,128)(2,1)} %broadcast_in_dim.177), calls=%async_computation | async-start | bytes 524288 | tf_op jit(solution)/shard_map/all_to_all | solution.py:30
  26.7 0.7 copy-start.2
  26.7 0.7 copy-start.3
  253.1 6.5 %copy-start = (f32[8,1,2,256]{3,2,1,0:T(2,128)S(1)}, f32[8,1,2,256]{3,2,1,0:T(2,128)}, u32[]{:S(2)}) copy-start(f32[8,1,2,256]{3,2,1,0:T(2,128)} %param.14) | copy-start | bytes 49156
  253.1 17.9 %all-to-all-start.1 = ((f32[32,8,1,2,256]{4,1,3,2,0:T(8,128)}), f32[32,8,1,2,256]{4,1,3,2,0:T(8,128)S(1)}, u32[]{:S(2)}, u32[]{:S(2)}) async-start(f32[32,8,1,2,256]{4,1,3,2,0:T(8,128)} %copy.178), calls=%async_computation.1 | async-start | bytes 1048576 | tf_op jit(solution)/shard_map/all_to_all | solution.py:44
  259.6 3.2 collective-permute-start
  259.7 3.2 collective-permute-start.1
  273.5 15.1 %all-to-all-start.2 = ((bf16[32,8,1,2,256]{4,1,3,2,0:T(8,128)(2,1)}), bf16[32,8,1,2,256]{4,1,3,2,0:T(8,128)(2,1)S(1)}, u32[]{:S(2)}, u32[]{:S(2)}) async-start(bf16[32,8,1,2,256]{4,1,3,2,0:T(8,128)(2,1)} %broadcast_in_dim.178), calls=%async_computation.2 | async-start | bytes 524288 | tf_op jit(solution)/shard_map/all_to_all | solution.py:30
  514.2 13.0 %all-to-all-start.4 = ((f32[32,2,1]{1,2,0:T(1,128)}), f32[32,2,1]{1,2,0:T(1,128)S(1)}, u32[]{:S(2)}, u32[]{:S(2)}) async-start(f32[32,2,1]{1,2,0:T(1,128)} %broadcast_in_dim.179), calls=%async_computation.4 | async-start | bytes 32768 | tf_op jit(solution)/shard_map/all_to_all | solution.py:30
  527.2 15.3 %all-to-all-start.3 = ((f32[32,8,1,2,256]{4,1,3,2,0:T(8,128)}), f32[32,8,1,2,256]{4,1,3,2,0:T(8,128)S(1)}, u32[]{:S(2)}, u32[]{:S(2)}) async-start(f32[32,8,1,2,256]{4,1,3,2,0:T(8,128)} %copy.200), calls=%async_computation.3 | async-start | bytes 1048576 | tf_op jit(solution)/shard_map/all_to_all | solution.py:44
  531.1 3.2 collective-permute-start.2
  531.1 3.2 collective-permute-start.3
where the time goes:
time: 551 us; the launch traced here: 545 us
  loops' own time  184 us (33%)
  local copies, waits for them, and re-layouts  143 us (26%)
  other arithmetic  96.7 us (18%)
  waiting for transfers between devices  42 us (8%)
  matrix products  40 us (7%)
  starting transfers between devices  37.8 us (7%)
    another operation x2, loops' own time, on_device(): grid_sum, misfit = lax.fori_loop(0, blocks_used[0], visit, initial)  184 us
    dynamic_update_slice x36, local copies, waits for them, and re-layouts, spoke_block(): return (lax.dynamic_update_slice(grid_sum, updated, corner), misfit)  81.8 us
    reduce_sum x36, other arithmetic, spoke_block(): misfit = jnp.sum(resid * resid)  48.9 us
    convert_element_type x36, other arithmetic, tap_matrix(): taps[offset].astype(jnp.float32)[:, None]  30.8 us
    dynamic_slice x36, local copies, waits for them, and re-layouts, visit(): lax.dynamic_index_in_dim(col_first[0], block_id, 0, keepdims=False)  25.3 us
    all_to_all x3, starting transfers between devices, sent_to_all(): return lax.all_to_all(copies, axis, split_axis=0, concat_axis=0, tiled=True)  23.9 us
    dynamic_slice x36, local copies, waits for them, and re-layouts, visit(): lax.dynamic_index_in_dim(col_offset[0], block_id, 0, keepdims=False)  23.5 us
    all_to_all x3, waiting for transfers between devices, sent_to_all(): return lax.all_to_all(copies, axis, split_axis=0, concat_axis=0, tiled=True)  23.5 us
  transfers between devices with their start and end apart: 9, of which 7 were waited for; matrix products, arithmetic and copies ran while one was open for 1% of the time, Pallas kernels for 0%

commit v1 on v0

v1 whole, which is shorter than its diff:
```python
import math

import jax
import jax.numpy as jnp
import numpy as np
from jax import lax
from jax.experimental import pallas as pl
from jax.experimental.pallas import tpu as pltpu
from jax.sharding import PartitionSpec as P

N = 256
NB = 18
BS = 256
KW = 4
ITERS = 2
GROUP = 2
NG = NB // GROUP
GS = GROUP * BS

step_size = 2.0
tv_weight = 0.1
smooth_floor = 0.5
shrink_weight = 0.1

f32 = jnp.float32
bf16 = jnp.bfloat16


def pair_tables(order):
    counter = np.arange(order)
    phase = (counter[:, None] * counter[None, :]) % order
    angle = phase.astype(np.float32) * np.float32(2.0 * math.pi / order)
    cosine = np.cos(angle) / np.float32(math.sqrt(order))
    sine = np.sin(angle) / np.float32(math.sqrt(order))
    forward = np.block([[cosine, sine], [-sine, cosine]])
    return jnp.asarray(forward, bf16), jnp.asarray(forward.T, bf16)


def vmem():
    return pl.BlockSpec(memory_space=pltpu.VMEM)


def smem():
    return pl.BlockSpec(memory_space=pltpu.SMEM)


def anywhere():
    return pl.BlockSpec(memory_space=pl.ANY)


def dot(left, right):
    return lax.dot_general(left, right, (((1,), (0,)), ((), ())), preferred_element_type=f32)


def dot_nt(left, right):
    return lax.dot_general(left, right, (((1,), (1,)), ((), ())), preferred_element_type=f32)


def start_kernel(image_ref, send_ref, rows_ref):
    real = image_ref[:, 0, 0, :]
    imag = image_ref[:, 0, 1, :]
    rows_ref[:, :N] = real
    rows_ref[:, N:] = imag
    low = jnp.concatenate([real, imag], axis=1).astype(bf16)
    send_ref[...] = jnp.broadcast_to(low[None], send_ref.shape)


def taps_kernel(count_ref, row_off_ref, col_off_ref, row_first_ref, col_first_ref, row_taps_ref, col_taps_ref, wx_ref, wy_ref):
    groups = (count_ref[0] + GROUP - 1) // GROUP
    position = lax.broadcasted_iota(jnp.int32, (N, BS), 0)

    def build(start, taps):
        matrix = jnp.zeros((N, BS), f32)
        for tap in range(KW):
            matrix = jnp.where(position == start + tap, taps[tap : tap + 1], matrix)
        return matrix.astype(bf16)

    def visit(group, carry):
        for member in range(GROUP):
            block = group * GROUP + member
            lanes = slice(member * BS, (member + 1) * BS)
            row_start = row_first_ref[0, pl.ds(block, 1), :] + row_off_ref[0, block]
            col_start = col_first_ref[0, pl.ds(block, 1), :] + col_off_ref[0, block]
            wx_ref[group, :, lanes] = build(row_start, row_taps_ref[0, block].astype(f32))
            wy_ref[group, :, lanes] = build(col_start, col_taps_ref[0, block].astype(f32))
        return carry

    lax.fori_loop(0, groups, visit, 0)


def pieces(value):
    high = value.astype(bf16)
    rest = value - high.astype(f32)
    middle = rest.astype(bf16)
    low = (rest - middle.astype(f32)).astype(bf16)
    return high.astype(f32), middle.astype(f32), low.astype(f32)


def coil_kernel(last, *refs):
    if last:
        (count_ref, image_ref, maps_ref, samples_ref, fwd_ref, adj_ref, wx_hbm, wy_hbm, before_ref) = refs[:9]
        (send_ref, wx_ref, wy_ref, grid_ref, sems) = refs[9:]
    else:
        (count_ref, image_ref, maps_ref, samples_ref, fwd_ref, adj_ref, wx_hbm, wy_hbm) = refs[:8]
        (send_ref, misfit_ref, wx_ref, wy_ref, grid_ref, sems) = refs[8:]
    count = count_ref[0]
    groups = (count + GROUP - 1) // GROUP

    def copies(group):
        return (
            pltpu.make_async_copy(wx_hbm.at[group], wx_ref.at[group], sems.at[0, group]),
            pltpu.make_async_copy(wy_hbm.at[group], wy_ref.at[group], sems.at[1, group]),
        )

    def fetch(group, carry):
        for copy in copies(group):
            copy.start()
        return carry

    lax.fori_loop(0, groups, fetch, 0)

    image = image_ref[...].astype(f32)
    real = image[:, :, :N].reshape(N, N)
    imag = image[:, :, N:].reshape(N, N)
    map_real = maps_ref[0, 0].astype(f32)
    map_imag = maps_ref[0, 1].astype(f32)
    coil_real = (map_real * real - map_imag * imag).astype(bf16)
    coil_imag = (map_real * imag + map_imag * real).astype(bf16)
    coil_image = jnp.concatenate([coil_real, coil_imag], axis=0)
    half = dot(fwd_ref[...], coil_image).astype(bf16)
    half = jnp.concatenate([half[:N], half[N:]], axis=1)
    kspace = dot_nt(fwd_ref[...], half).astype(bf16)
    grid_ref[...] = jnp.zeros_like(grid_ref)

    def visit(group, misfit):
        for copy in copies(group):
            copy.wait()
        wx = wx_ref[group]
        wy = wy_ref[group]
        wy_wide = wy.astype(f32)
        across = dot(kspace, wx)
        weighted = []
        for part in range(2):
            predicted = jnp.sum(across[part * N : (part + 1) * N] * wy_wide, axis=0, keepdims=True)
            resid = []
            for member in range(GROUP):
                block = group * GROUP + member
                measured = samples_ref[0, 0, block].astype(f32)[part : part + 1]
                off = predicted[:, member * BS : (member + 1) * BS] - measured
                resid.append(jnp.where(block < count, off, 0.0))
            resid = jnp.concatenate(resid, axis=1)
            misfit = misfit + resid * resid
            weighted.append(wy * resid.astype(bf16))
        weighted = jnp.concatenate(weighted, axis=0)
        grid_ref[...] += dot_nt(weighted, wx)
        return misfit

    misfit = lax.fori_loop(0, groups, visit, jnp.zeros((1, GS), f32))
    misfit = jnp.broadcast_to(jnp.sum(misfit, axis=1, keepdims=True), (8, 128))

    grid = grid_ref[...].astype(bf16)
    grid = jnp.concatenate([grid[:N], grid[N:]], axis=1)
    back_half = dot_nt(adj_ref[...], grid).astype(bf16)
    back_half = jnp.concatenate([back_half[:N], back_half[N:]], axis=1)
    back = dot(back_half, fwd_ref[...])
    back_real = back[:, :N]
    back_imag = back[:, N:]
    out_real = map_real * back_real + map_imag * back_imag
    out_imag = map_real * back_imag - map_imag * back_real
    parts = send_ref.shape[0]
    send_ref[:, :, :N] = out_real.reshape(parts, -1, N).astype(bf16)
    send_ref[:, :, N : 2 * N] = out_imag.reshape(parts, -1, N).astype(bf16)
    if last:
        row = lax.broadcasted_iota(jnp.int32, (8, 128), 0)
        extra = jnp.zeros((8, 128), f32)
        for place, piece in enumerate(pieces(before_ref[...]) + pieces(misfit)):
            extra = jnp.where(row == place, piece, extra)
        send_ref[:, :, 2 * N :] = jnp.broadcast_to(extra.astype(bf16)[None], (parts, 8, 128))
    else:
        misfit_ref[...] = misfit


def shrunk(detail, limit):
    real = detail[:, :N]
    imag = detail[:, N:]
    length = jnp.sqrt(real * real + imag * imag)
    factor = jnp.maximum(length - limit, 0.0) / jnp.maximum(length, limit)
    return detail * jnp.concatenate([factor, factor], axis=1)


def unit_change(change):
    real = change[:, :N]
    imag = change[:, N:]
    length = jnp.sqrt(real * real + imag * imag + smooth_floor * smooth_floor)
    return change / jnp.concatenate([length, length], axis=1)


def update_kernel(last, carry_on, misfit_scale, *refs):
    if last:
        (parts_ref, moving_ref, left_ref, right_ref, image_ref, misfit_ref) = refs
    else:
        (parts_ref, moving_ref, left_ref, right_ref, current_ref, send_ref, updated_ref, next_ref) = refs
    total = jnp.sum(parts_ref[...].astype(f32), axis=0)
    moving = moving_ref[...]
    tv_grad = unit_change(moving - left_ref[...]) - unit_change(right_ref[...] - moving)
    field = moving - step_size * (total[:, : 2 * N] + tv_weight * tv_grad)
    rows, width = field.shape
    row_even = lax.broadcasted_iota(jnp.int32, field.shape, 0) % 2 == 0
    col_even = lax.broadcasted_iota(jnp.int32, field.shape, 1) % 2 == 0
    beside = jnp.where(col_even, pltpu.roll(field, width - 1, 1), pltpu.roll(field, 1, 1))
    col_sum = field + beside
    col_diff = jnp.where(col_even, field - beside, beside - field)

    def other_row(values):
        return jnp.where(row_even, pltpu.roll(values, rows - 1, 0), pltpu.roll(values, 1, 0))

    sum_other = other_row(col_sum)
    diff_other = other_row(col_diff)
    limit = step_size * shrink_weight
    approx = (col_sum + sum_other) * 0.5
    horiz = shrunk((col_diff + diff_other) * 0.5, limit)
    vertical = shrunk(jnp.where(row_even, col_sum - sum_other, sum_other - col_sum) * 0.5, limit)
    diagonal = shrunk(jnp.where(row_even, col_diff - diff_other, diff_other - col_diff) * 0.5, limit)
    across = jnp.where(row_even, horiz + diagonal, horiz - diagonal)
    along = jnp.where(row_even, approx + vertical, approx - vertical)
    updated = jnp.where(col_even, along + across, along - across) * 0.5
    if last:
        image_ref[:, 0, 0, :] = updated[:, :N]
        image_ref[:, 0, 1, :] = updated[:, N:]
        extra = total[:, 2 * N :] * misfit_scale
        misfit_ref[0:1, :] = jnp.sum(extra[0:3], axis=0, keepdims=True)
        misfit_ref[1:2, :] = jnp.sum(extra[3:6], axis=0, keepdims=True)
    else:
        following = updated + carry_on * (updated - current_ref[...])
        updated_ref[...] = updated
        next_ref[...] = following
        send_ref[...] = jnp.broadcast_to(following.astype(bf16)[None], send_ref.shape)


def exchanged(parts):
    return lax.all_to_all(parts, "coil", 0, 0, tiled=True)


def neighbours(values):
    count = lax.axis_size("frame")
    left = lax.ppermute(values, "frame", [(i, (i + 1) % count) for i in range(count)])
    right = lax.ppermute(values, "frame", [((i + 1) % count, i) for i in range(count)])
    return left, right


def on_device(
    initial_image,
    coil_maps,
    samples,
    blocks_used,
    row_offset,
    col_offset,
    row_first,
    col_first,
    row_taps,
    col_taps,
):
    coils = lax.axis_size("coil")
    rows = initial_image.shape[0]
    misfit_scale = 0.5 / (coil_maps.shape[0] * coils * NB * BS)
    forward, adjoint = pair_tables(N)
    params = pltpu.CompilerParams(vmem_limit_bytes=32 * 1024 * 1024)
    shape = jax.ShapeDtypeStruct
    send_shape = shape((coils, rows, 2 * N), bf16)
    rows_shape = shape((rows, 2 * N), f32)

    send, moving = pl.pallas_call(
        start_kernel,
        out_shape=(send_shape, rows_shape),
        in_specs=[vmem()],
        out_specs=(vmem(), vmem()),
        compiler_params=params,
        name="start",
    )(initial_image)
    current = moving

    wx, wy = pl.pallas_call(
        taps_kernel,
        out_shape=(shape((NG, N, GS), bf16), shape((NG, N, GS), bf16)),
        in_specs=[smem(), smem(), smem(), vmem(), vmem(), vmem(), vmem()],
        out_specs=(vmem(), vmem()),
        compiler_params=params,
        name="taps",
    )(blocks_used, row_offset, col_offset, row_first, col_first, row_taps, col_taps)

    momentum = 1.0
    misfit = None
    for step_num in range(ITERS):
        last = step_num == ITERS - 1
        gathered = exchanged(send)
        left, right = neighbours(moving)
        if step_num == 0:
            gathered, left, right, wx, wy = lax.optimization_barrier((gathered, left, right, wx, wy))
        else:
            gathered, left, right = lax.optimization_barrier((gathered, left, right))
        inputs = [blocks_used, gathered, coil_maps, samples, forward, adjoint, wx, wy]
        specs = [smem(), vmem(), vmem(), vmem(), vmem(), vmem(), anywhere(), anywhere()]
        if last:
            inputs.append(misfit)
            specs.append(vmem())
            out_shape = (shape((coils, rows, 2 * N + 128), bf16),)
        else:
            out_shape = (send_shape, shape((8, 128), f32))
        results = pl.pallas_call(
            lambda *refs, last=last: coil_kernel(last, *refs),
            out_shape=out_shape,
            in_specs=specs,
            out_specs=tuple(vmem() for _ in out_shape),
            scratch_shapes=[
                pltpu.VMEM((NG, N, GS), bf16),
                pltpu.VMEM((NG, N, GS), bf16),
                pltpu.VMEM((2 * N, N), f32),
                pltpu.SemaphoreType.DMA((2, NG)),
            ],
            compiler_params=params,
            name=f"coil{step_num}",
        )(*inputs)
        partial = results[0]
        if not last:
            misfit = results[1]
        parts = exchanged(partial)
        following = (1.0 + math.sqrt(1.0 + 4.0 * momentum * momentum)) / 2.0
        carry_on = (momentum - 1.0) / following
        inputs = [parts, moving, left, right]
        if last:
            out_shape = (shape(initial_image.shape, f32), shape((ITERS, 128), f32))
        else:
            inputs.append(current)
            out_shape = (send_shape, rows_shape, rows_shape)
        results = pl.pallas_call(
            lambda *refs, last=last, carry_on=carry_on: update_kernel(last, carry_on, misfit_scale, *refs),
            out_shape=out_shape,
            in_specs=[vmem() for _ in inputs],
            out_specs=tuple(vmem() for _ in out_shape),
            compiler_params=params,
            name=f"update{step_num}",
        )(*inputs)
        if last:
            image, misfit_rows = results
        else:
            send, current, moving = results
        momentum = following
    return image, misfit_rows[:, :1]


def solution(mesh):
    placed = (
        P("coil", "frame", None, None),
        P("coil", None, None, None),
        P("coil", "frame", None, None, None),
        P("frame"),
        P("frame", None),
        P("frame", None),
        P("frame", None, None),
        P("frame", None, None),
        P("frame", None, None, None),
        P("frame", None, None, None),
    )
    return jax.shard_map(
        on_device,
        mesh=mesh,
        in_specs=placed,
        out_specs=(P("coil", "frame", None, None), P(None, "frame")),
        check_vma=False,
    )
```

time: 551 us -> 106 us (0.19)
  the two profiles are of different devices: /device:TPU:1 before, /device:TPU:64 now
where the time goes in v1:
time: 106 us; the launch traced here: 105 us
  blocking collectives  39.9 us (38%)
  starting transfers between devices  26.2 us (25%)
  local copies, waits for them, and re-layouts  17.4 us (16%)
  Pallas kernels  10.1 us (10%)
  waiting for transfers between devices  9.61 us (9%)
  between operations  1.37 us (1%)
    all_to_all x2, blocking collectives, exchanged(): return lax.all_to_all(parts, 'coil', 0, 0, tiled=True)  39.9 us
    all_to_all x2, starting transfers between devices, exchanged(): return lax.all_to_all(parts, 'coil', 0, 0, tiled=True)  17.7 us
    unnamed x41, local copies, waits for them, and re-layouts  17.4 us
    ppermute x2, starting transfers between devices, neighbours(): lax.ppermute(values, 'frame', [((i + 1) % count, i) for i in range(count)])  8.51 us
    pallas_call x2, Pallas kernels, on_device(): pl.pallas_call(lambda *refs, last=last: coil_kernel(last, *refs), out_sha...  6.56 us
    all_to_all x2, waiting for transfers between devices, exchanged(): return lax.all_to_all(parts, 'coil', 0, 0, tiled=True)  5.24 us
    ppermute x2, waiting for transfers between devices, neighbours(): lax.ppermute(values, 'frame', [(i, (i + 1) % count) for i in range(count)])  2.93 us
  transfers between devices with their start and end apart: 6, of which 4 were waited for; matrix products, arithmetic and copies ran while one was open for 1% of the time, Pallas kernels for 1%

profile of v1, /device:TPU:64, one launch (start us, length us, event | category | flops | bytes accessed | tf_op | source)
XLA Modules:
  0.0 104.6 jit_solution(11143833648248644750)
XLA Ops:
  0.6 0.0 copy-start.16
  0.6 0.7 copy-done.16
  1.3 0.7 start.1
  2.1 12.6 %all-to-all-start = ((bf16[32,8,512]{2,1,0:T(8,128)(2,1)}), bf16[32,8,512]{2,1,0:T(8,128)(2,1)S(1)}, u32[]{:S(2)}, u32[]{:S(2)}) async-start(bf16[32,8,512]{2,1,0:T(8,128)(2,1)} %get-tuple-element.20), calls=%async_computation | async-start | bytes 524288 | tf_op jit(solution)/shard_map/all_to_all | solution.py:241
  14.7 2.4 %collective-permute-start.1 = (f32[8,512]{1,0:T(8,128)S(1)}, f32[8,512]{1,0:T(8,128)S(1)}, u32[]{:S(2)}, u32[]{:S(2)}) collective-permute-start(f32[8,512]{1,0:T(8,128)S(1)} %get-tuple-element.21.refs_1_.refs_4_), channel_id=1, source_target_pairs={{1,0},{2,1},{3,2},{4,3},{5,4},{6,5},{7,6},{8,7},{9,8},{10,9},{11,1... | collective-permute-start | bytes 49160 | tf_op jit(solution)/shard_map/ppermute | solution.py:247
  17.0 0.0 collective-permute-start
  17.7 0.7 copy.14.row_first_ref
  18.4 0.7 copy.15.col_first_ref
  19.2 0.0 copy-start.14
  19.2 0.8 copy-done.14
  19.9 0.0 copy-start.15
  19.9 0.8 copy-done.15
  20.7 0.0 copy-start.17
  20.7 0.7 copy-done.17
  21.3 0.7 copy-done.18
  22.0 1.2 %taps.1 = (bf16[9,256,512]{2,1,0:T(8,128)(2,1)S(1)}, bf16[9,256,512]{2,1,0:T(8,128)(2,1)S(1)}) custom-call(s32[1]{0:T(128)S(6)} %copy.17.count_ref.refs_0_, s32[1,18]{1,0:T(1,128)S(1)} %copy-done.17, s32[1,18]{1,0:T(1,128)S(1)} %copy-done.18, s32[1,18,256]{2,1,0:T(8,128)S(1)} %copy.14.row_first_ref, s32[1,18,256]{2,1,0:T(8,128)S(1)} %copy.15.col_first_ref, ...), custom_call_target="tpu_custom_call" | custom-call | tf_op jit(solution)/shard_map/taps/pallas_call | solution.py:282
  23.2 0.0 copy-start
  23.2 1.4 %copy-done = bf16[9,256,512]{2,1,0:T(8,128)(2,1)} copy-done((bf16[9,256,512]{2,1,0:T(8,128)(2,1)}, bf16[9,256,512]{2,1,0:T(8,128)(2,1)S(1)}, u32[]{:S(2)}) %copy-start) | copy-done | bytes 2359320
  24.6 0.0 collective-permute-done.1.refs_3_
  24.6 0.0 collective-permute-done.refs_2_
  24.6 2.4 %all-to-all-done.refs_1_ = bf16[32,8,512]{2,1,0:T(8,128)(2,1)S(1)} async-done(((bf16[32,8,512]{2,1,0:T(8,128)(2,1)}), bf16[32,8,512]{2,1,0:T(8,128)(2,1)S(1)}, u32[]{:S(2)}, u32[]{:S(2)}) %all-to-all-start) | async-done | bytes 262176 | tf_op jit(solution)/shard_map/all_to_all | solution.py:241
  27.0 0.7 copy-done.9
  27.7 1.7 %copy-done.1 = bf16[9,256,512]{2,1,0:T(8,128)(2,1)S(1)} copy-done((bf16[9,256,512]{2,1,0:T(8,128)(2,1)S(1)}, bf16[9,256,512]{2,1,0:T(8,128)(2,1)}, u32[]{:S(2)}) %copy-start.1) | copy-done | bytes 2359320
  29.3 1.0 copy-done.3
  30.4 1.0 copy-done.5
  31.4 0.9 copy-done.7
  32.4 0.9 copy-done.10
  33.3 0.7 copy-done.12
  34.1 2.8 %coil0.1 = (bf16[32,8,512]{2,1,0:T(8,128)(2,1)S(1)}, f32[8,128]{1,0:T(8,128)S(1)}) custom-call(s32[1]{0:T(128)S(6)} %copy.17.count_ref.refs_0_, bf16[32,8,512]{2,1,0:T(8,128)(2,1)S(1)} %copy-done.10, bf16[1,2,256,256]{3,2,1,0:T(8,128)(2,1)S(1)} %copy-done.7, bf16[1,1,18,2,256]{4,3,2,1,0:T(2,128)(2,1)S(1)} %copy-done.12, bf16[512,512]{1,0:T(8,128)(2,1)S(1)} %copy-done.5, ...), custom_call_target="tpu_custom_call" | custom-call | tf_op jit(solution)/shard_map/coil0/pallas_call | solution.py:309
  36.9 19.2 %all_to_all.20.refs_0_ = bf16[32,8,512]{2,1,0:T(8,128)(2,1)S(1)} all-to-all(bf16[32,8,512]{2,1,0:T(8,128)(2,1)S(1)} %get-tuple-element.27), channel_id=1, replica_groups=mesh['coil'=32,'frame'=16] {'coil'}, dimensions={0} | all-to-all | bytes 524288 | tf_op jit(solution)/shard_map/all_to_all | solution.py:241
  56.1 0.8 update0.1
  56.9 0.7 copy-done.11
  57.6 5.1 %all-to-all-start.2 = ((bf16[32,8,512]{2,1,0:T(8,128)(2,1)}), bf16[32,8,512]{2,1,0:T(8,128)(2,1)}, u32[]{:S(2)}, u32[]{:S(2)}) async-start(bf16[32,8,512]{2,1,0:T(8,128)(2,1)} %copy-done.11), calls=%async_computation.2 | async-start | bytes 524288 | tf_op jit(solution)/shard_map/all_to_all | solution.py:241
  62.7 6.1 %collective-permute-start.3 = (f32[8,512]{1,0:T(8,128)S(1)}, f32[8,512]{1,0:T(8,128)S(1)}, u32[]{:S(2)}, u32[]{:S(2)}) collective-permute-start(f32[8,512]{1,0:T(8,128)S(1)} %get-tuple-element.31.refs_1_), channel_id=1, source_target_pairs={{1,0},{2,1},{3,2},{4,3},{5,4},{6,5},{7,6},{8,7},{9,8},{10,9},{11,1... | collective-permute-start | bytes 49160 | tf_op jit(solution)/shard_map/ppermute | solution.py:247
  68.8 0.0 collective-permute-start.2
  68.8 1.4 %collective-permute-done.3.refs_3_ = f32[8,512]{1,0:T(8,128)S(1)} collective-permute-done((f32[8,512]{1,0:T(8,128)S(1)}, f32[8,512]{1,0:T(8,128)S(1)}, u32[]{:S(2)}, u32[]{:S(2)}) %collective-permute-start.3) | collective-permute-done | bytes 16416 | tf_op jit(solution)/shard_map/ppermute | solution.py:247
  70.3 2.9 %collective-permute-done.2.refs_2_ = f32[8,512]{1,0:T(8,128)S(1)} collective-permute-done((f32[8,512]{1,0:T(8,128)S(1)}, f32[8,512]{1,0:T(8,128)S(1)}, u32[]{:S(2)}, u32[]{:S(2)}) %collective-permute-start.2) | collective-permute-done | bytes 16416 | tf_op jit(solution)/shard_map/ppermute | solution.py:246
  73.2 2.9 %all-to-all-done.2.refs_1_ = bf16[32,8,512]{2,1,0:T(8,128)(2,1)} async-done(((bf16[32,8,512]{2,1,0:T(8,128)(2,1)}), bf16[32,8,512]{2,1,0:T(8,128)(2,1)}, u32[]{:S(2)}, u32[]{:S(2)}) %all-to-all-start.2) | async-done | bytes 262176 | tf_op jit(solution)/shard_map/all_to_all | solution.py:241
  76.1 0.0 copy-done.4
  76.1 0.0 copy-done.6
  76.1 0.0 copy-done.13
  76.1 0.0 copy-start.2
  76.1 1.7 %copy-done.2 = bf16[9,256,512]{2,1,0:T(8,128)(2,1)S(1)} copy-done((bf16[9,256,512]{2,1,0:T(8,128)(2,1)S(1)}, bf16[9,256,512]{2,1,0:T(8,128)(2,1)}, u32[]{:S(2)}) %copy-start.2) | copy-done | bytes 2359320
  77.8 0.9 copy-done.8
  78.7 3.8 %coil1.1 = bf16[32,8,640]{2,1,0:T(8,128)(2,1)S(1)} custom-call(s32[1]{0:T(128)S(6)} %copy.17.count_ref.refs_0_, bf16[32,8,512]{2,1,0:T(8,128)(2,1)} %all-to-all-done.2.refs_1_, bf16[1,2,256,256]{3,2,1,0:T(8,128)(2,1)S(1)} %copy-done.8, bf16[1,1,18,2,256]{4,3,2,1,0:T(2,128)(2,1)S(1)} %copy-done.13, bf16[512,512]{1,0:T(8,128)(2,1)S(1)} %copy-done.6, ...), custom_call_target="tpu_custom_call" | custom-call | tf_op jit(solution)/shard_map/coil1/pallas_call | solution.py:309
  82.5 20.7 %all_to_all.21.refs_0_ = bf16[32,8,640]{2,1,0:T(8,128)(2,1)S(1)} all-to-all(bf16[32,8,640]{2,1,0:T(8,128)(2,1)S(1)} %coil1.1), channel_id=1, replica_groups=mesh['coil'=32,'frame'=16] {'coil'}, dimensions={0} | all-to-all | bytes 655360 | tf_op jit(solution)/shard_map/all_to_all | solution.py:241
  103.2 0.8 update1.1
  104.0 0.6 copy.16
  (13 shorter events, 0.0 us)
Async XLA Ops:
  0.6 0.7 copy-start.16
  2.1 24.9 %all-to-all-start = ((bf16[32,8,512]{2,1,0:T(8,128)(2,1)}), bf16[32,8,512]{2,1,0:T(8,128)(2,1)S(1)}, u32[]{:S(2)}, u32[]{:S(2)}) async-start(bf16[32,8,512]{2,1,0:T(8,128)(2,1)} %get-tuple-element.20), calls=%async_computation | async-start | bytes 524288 | tf_op jit(solution)/shard_map/all_to_all | solution.py:241
  14.7 9.9 %collective-permute-start.1 = (f32[8,512]{1,0:T(8,128)S(1)}, f32[8,512]{1,0:T(8,128)S(1)}, u32[]{:S(2)}, u32[]{:S(2)}) collective-permute-start(f32[8,512]{1,0:T(8,128)S(1)} %get-tuple-element.21.refs_1_.refs_4_), channel_id=1, source_target_pairs={{1,0},{2,1},{3,2},{4,3},{5,4},{6,5},{7,6},{8,7},{9,8},{10,9},{11,1... | collective-permute-start | bytes 49160 | tf_op jit(solution)/shard_map/ppermute | solution.py:247
  17.0 7.6 %collective-permute-start = (f32[8,512]{1,0:T(8,128)S(1)}, f32[8,512]{1,0:T(8,128)S(1)}, u32[]{:S(2)}, u32[]{:S(2)}) collective-permute-start(f32[8,512]{1,0:T(8,128)S(1)} %get-tuple-element.21.refs_1_.refs_4_), channel_id=1, source_target_pairs={{0,1},{1,2},{2,3},{3,4},{4,5},{5,6},{6,7},{7,8},{8,9},{9,10},{10,1... | collective-permute-start | bytes 49160 | tf_op jit(solution)/shard_map/ppermute | solution.py:246
  19.2 0.8 copy-start.14
  19.9 0.8 copy-start.15
  20.7 0.7 copy-start.17
  21.3 0.7 copy-start.18
  23.2 1.4 %copy-start = (bf16[9,256,512]{2,1,0:T(8,128)(2,1)}, bf16[9,256,512]{2,1,0:T(8,128)(2,1)S(1)}, u32[]{:S(2)}) copy-start(bf16[9,256,512]{2,1,0:T(8,128)(2,1)S(1)} %get-tuple-element.26.refs_7_) | copy-start | bytes 7077892
  27.0 0.7 copy-start.9
  27.7 1.7 %copy-start.1 = (bf16[9,256,512]{2,1,0:T(8,128)(2,1)S(1)}, bf16[9,256,512]{2,1,0:T(8,128)(2,1)}, u32[]{:S(2)}) copy-start(bf16[9,256,512]{2,1,0:T(8,128)(2,1)} %copy-done) | copy-start | bytes 7077892
  29.3 1.0 copy-start.3
  30.4 1.0 copy-start.5
  31.4 0.9 copy-start.7
  32.4 0.9 copy-start.10
  33.3 0.7 copy-start.12
  34.0 42.1 %copy-start.4 = (bf16[512,512]{1,0:T(8,128)(2,1)S(1)}, bf16[512,512]{1,0:T(8,128)(2,1)}, u32[]{:S(2)}) copy-start(bf16[512,512]{1,0:T(8,128)(2,1)} %constant.5.clone.refs_5_) | copy-start | bytes 1572868
  34.1 42.1 %copy-start.6 = (bf16[512,512]{1,0:T(8,128)(2,1)S(1)}, bf16[512,512]{1,0:T(8,128)(2,1)}, u32[]{:S(2)}) copy-start(bf16[512,512]{1,0:T(8,128)(2,1)} %constant.4.clone.refs_4_) | copy-start | bytes 1572868
  34.1 42.1 %copy-start.13 = (bf16[1,1,18,2,256]{4,3,2,1,0:T(2,128)(2,1)S(1)}, bf16[1,1,18,2,256]{4,3,2,1,0:T(2,128)(2,1)}, u32[]{:S(2)}) copy-start(bf16[1,1,18,2,256]{4,3,2,1,0:T(2,128)(2,1)} %refs_3_.3) | copy-start | bytes 55300
  56.9 0.7 copy-start.11
  57.6 18.5 %all-to-all-start.2 = ((bf16[32,8,512]{2,1,0:T(8,128)(2,1)}), bf16[32,8,512]{2,1,0:T(8,128)(2,1)}, u32[]{:S(2)}, u32[]{:S(2)}) async-start(bf16[32,8,512]{2,1,0:T(8,128)(2,1)} %copy-done.11), calls=%async_computation.2 | async-start | bytes 524288 | tf_op jit(solution)/shard_map/all_to_all | solution.py:241
  62.7 7.6 %collective-permute-start.3 = (f32[8,512]{1,0:T(8,128)S(1)}, f32[8,512]{1,0:T(8,128)S(1)}, u32[]{:S(2)}, u32[]{:S(2)}) collective-permute-start(f32[8,512]{1,0:T(8,128)S(1)} %get-tuple-element.31.refs_1_), channel_id=1, source_target_pairs={{1,0},{2,1},{3,2},{4,3},{5,4},{6,5},{7,6},{8,7},{9,8},{10,9},{11,1... | collective-permute-start | bytes 49160 | tf_op jit(solution)/shard_map/ppermute | solution.py:247
  68.8 4.4 %collective-permute-start.2 = (f32[8,512]{1,0:T(8,128)S(1)}, f32[8,512]{1,0:T(8,128)S(1)}, u32[]{:S(2)}, u32[]{:S(2)}) collective-permute-start(f32[8,512]{1,0:T(8,128)S(1)} %get-tuple-element.31.refs_1_), channel_id=1, source_target_pairs={{0,1},{1,2},{2,3},{3,4},{4,5},{5,6},{6,7},{7,8},{8,9},{9,10},{10,1... | collective-permute-start | bytes 49160 | tf_op jit(solution)/shard_map/ppermute | solution.py:246
  76.1 1.7 %copy-start.2 = (bf16[9,256,512]{2,1,0:T(8,128)(2,1)S(1)}, bf16[9,256,512]{2,1,0:T(8,128)(2,1)}, u32[]{:S(2)}) copy-start(bf16[9,256,512]{2,1,0:T(8,128)(2,1)} %copy-done) | copy-start | bytes 7077892
  77.8 0.9 copy-start.8

commit v2 on v1

--- a/solution.py
+++ b/solution.py
@@ -26,14 +26,13 @@
 bf16 = jnp.bfloat16
 
 
-def pair_tables(order):
+def pair_table(order):
     counter = np.arange(order)
     phase = (counter[:, None] * counter[None, :]) % order
     angle = phase.astype(np.float32) * np.float32(2.0 * math.pi / order)
     cosine = np.cos(angle) / np.float32(math.sqrt(order))
     sine = np.sin(angle) / np.float32(math.sqrt(order))
-    forward = np.block([[cosine, sine], [-sine, cosine]])
-    return jnp.asarray(forward, bf16), jnp.asarray(forward.T, bf16)
+    return jnp.asarray(np.block([[cosine, sine], [-sine, cosine]]), bf16)
 
 
 def vmem():
@@ -44,8 +43,12 @@
     return pl.BlockSpec(memory_space=pltpu.SMEM)
 
 
-def anywhere():
-    return pl.BlockSpec(memory_space=pl.ANY)
+def hbm():
+    return pl.BlockSpec(memory_space=pltpu.HBM)
+
+
+def in_hbm(values):
+    return pltpu.with_memory_space_constraint(values, pltpu.HBM)
 
 
 def dot(left, right):
@@ -56,7 +59,10 @@
     return lax.dot_general(left, right, (((1,), (1,)), ((), ())), preferred_element_type=f32)
 
 
-def start_kernel(image_ref, send_ref, rows_ref):
+def start_kernel(image_hbm, send_ref, rows_ref, image_ref, sem):
+    copy = pltpu.make_async_copy(image_hbm, image_ref, sem)
+    copy.start()
+    copy.wait()
     real = image_ref[:, 0, 0, :]
     imag = image_ref[:, 0, 1, :]
     rows_ref[:, :N] = real
@@ -65,27 +71,53 @@
     send_ref[...] = jnp.broadcast_to(low[None], send_ref.shape)
 
 
-def taps_kernel(count_ref, row_off_ref, col_off_ref, row_first_ref, col_first_ref, row_taps_ref, col_taps_ref, wx_ref, wy_ref):
+def taps_kernel(count_ref, *refs):
+    sources, (wx_hbm, wy_hbm), kept, held = refs[:9], refs[9:11], refs[11:14], refs[14:20]
+    wx_ref, wy_ref, in_sems, out_sems = refs[20:]
+    row_off, col_off, row_first, col_first, row_taps, col_taps = held
+    loads = [pltpu.make_async_copy(source, own, in_sems.at[k]) for k, (source, own) in enumerate(zip(sources, held + kept))]
+    for load in loads:
+        load.start()
+    for load in loads[: len(held)]:
+        load.wait()
     groups = (count_ref[0] + GROUP - 1) // GROUP
     position = lax.broadcasted_iota(jnp.int32, (N, BS), 0)
 
+    def stores(group):
+        return (
+            pltpu.make_async_copy(wx_ref.at[group], wx_hbm.at[group], out_sems.at[0, group]),
+            pltpu.make_async_copy(wy_ref.at[group], wy_hbm.at[group], out_sems.at[1, group]),
+        )
+
     def build(start, taps):
+        offset = position - start
         matrix = jnp.zeros((N, BS), f32)
         for tap in range(KW):
-            matrix = jnp.where(position == start + tap, taps[tap : tap + 1], matrix)
+            matrix = jnp.where(offset == tap, taps[tap : tap + 1], matrix)
         return matrix.astype(bf16)
 
     def visit(group, carry):
         for member in range(GROUP):
             block = group * GROUP + member
             lanes = slice(member * BS, (member + 1) * BS)
-            row_start = row_first_ref[0, pl.ds(block, 1), :] + row_off_ref[0, block]
-            col_start = col_first_ref[0, pl.ds(block, 1), :] + col_off_ref[0, block]
-            wx_ref[group, :, lanes] = build(row_start, row_taps_ref[0, block].astype(f32))
-            wy_ref[group, :, lanes] = build(col_start, col_taps_ref[0, block].astype(f32))
+            row_start = row_first[block] + row_off[0, block]
+            col_start = col_first[block] + col_off[0, block]
+            wx_ref[group, :, lanes] = build(row_start, row_taps[0, block].astype(f32))
+            wy_ref[group, :, lanes] = build(col_start, col_taps[0, block].astype(f32))
+        for store in stores(group):
+            store.start()
         return carry
 
     lax.fori_loop(0, groups, visit, 0)
+
+    def finish(group, carry):
+        for store in stores(group):
+            store.wait()
+        return carry
+
+    lax.fori_loop(0, groups, finish, 0)
+    for load in loads[len(held) :]:
+        load.wait()
 
 
 def pieces(value):
@@ -98,11 +130,11 @@
 
 def coil_kernel(last, *refs):
     if last:
-        (count_ref, image_ref, maps_ref, samples_ref, fwd_ref, adj_ref, wx_hbm, wy_hbm, before_ref) = refs[:9]
-        (send_ref, wx_ref, wy_ref, grid_ref, sems) = refs[9:]
+        (count_ref, image_ref, maps_ref, samples_ref, fwd_ref, wx_hbm, wy_hbm, before_ref) = refs[:8]
+        (send_ref, wx_ref, wy_ref, grid_ref, sems) = refs[8:]
     else:
-        (count_ref, image_ref, maps_ref, samples_ref, fwd_ref, adj_ref, wx_hbm, wy_hbm) = refs[:8]
-        (send_ref, misfit_ref, wx_ref, wy_ref, grid_ref, sems) = refs[8:]
+        (count_ref, image_ref, maps_ref, samples_ref, fwd_ref, wx_hbm, wy_hbm) = refs[:7]
+        (send_ref, misfit_ref, wx_ref, wy_ref, grid_ref, sems) = refs[7:]
     count = count_ref[0]
     groups = (count + GROUP - 1) // GROUP
 
@@ -158,10 +190,9 @@
     misfit = lax.fori_loop(0, groups, visit, jnp.zeros((1, GS), f32))
     misfit = jnp.broadcast_to(jnp.sum(misfit, axis=1, keepdims=True), (8, 128))
 
-    grid = grid_ref[...].astype(bf16)
-    grid = jnp.concatenate([grid[:N], grid[N:]], axis=1)
-    back_half = dot_nt(adj_ref[...], grid).astype(bf16)
-    back_half = jnp.concatenate([back_half[:N], back_half[N:]], axis=1)
+    grid = jnp.concatenate([grid_ref[:N].astype(bf16), -grid_ref[N:].astype(bf16)], axis=1)
+    back_half = dot_nt(fwd_ref[...], grid)
+    back_half = jnp.concatenate([back_half[:N].astype(bf16), -back_half[N:].astype(bf16)], axis=1)
     back = dot(back_half, fwd_ref[...])
     back_real = back[:, :N]
     back_imag = back[:, N:]
@@ -228,8 +259,10 @@
         image_ref[:, 0, 0, :] = updated[:, :N]
         image_ref[:, 0, 1, :] = updated[:, N:]
         extra = total[:, 2 * N :] * misfit_scale
-        misfit_ref[0:1, :] = jnp.sum(extra[0:3], axis=0, keepdims=True)
-        misfit_ref[1:2, :] = jnp.sum(extra[3:6], axis=0, keepdims=True)
+        first = jnp.sum(extra[0:3], axis=0, keepdims=True)
+        second = jnp.sum(extra[3:6], axis=0, keepdims=True)
+        lane = lax.broadcasted_iota(jnp.int32, first.shape, 1)
+        misfit_ref[...] = jnp.where(lane == 0, first, second)[:, :ITERS]
     else:
         following = updated + carry_on * (updated - current_ref[...])
         updated_ref[...] = updated
@@ -263,7 +296,7 @@
     coils = lax.axis_size("coil")
     rows = initial_image.shape[0]
     misfit_scale = 0.5 / (coil_maps.shape[0] * coils * NB * BS)
-    forward, adjoint = pair_tables(N)
+    forward = pair_table(N)
     params = pltpu.CompilerParams(vmem_limit_bytes=32 * 1024 * 1024)
     shape = jax.ShapeDtypeStruct
     send_shape = shape((coils, rows, 2 * N), bf16)
@@ -272,21 +305,46 @@
     send, moving = pl.pallas_call(
         start_kernel,
         out_shape=(send_shape, rows_shape),
-        in_specs=[vmem()],
+        in_specs=[hbm()],
         out_specs=(vmem(), vmem()),
+        scratch_shapes=[pltpu.VMEM(initial_image.shape, f32), pltpu.SemaphoreType.DMA],
         compiler_params=params,
         name="start",
-    )(initial_image)
+    )(in_hbm(initial_image))
     current = moving
 
-    wx, wy = pl.pallas_call(
+    firsts = (NB, 1, BS)
+    weights = pltpu.VMEM((NG, N, GS), bf16)
+    wx, wy, forward, maps, measured = pl.pallas_call(
         taps_kernel,
-        out_shape=(shape((NG, N, GS), bf16), shape((NG, N, GS), bf16)),
-        in_specs=[smem(), smem(), smem(), vmem(), vmem(), vmem(), vmem()],
-        out_specs=(vmem(), vmem()),
+        out_shape=(
+            pltpu.HBM((NG, N, GS), bf16),
+            pltpu.HBM((NG, N, GS), bf16),
+            pltpu.VMEM(forward.shape, bf16),
+            pltpu.VMEM(coil_maps.shape, bf16),
+            pltpu.VMEM(samples.shape, bf16),
+        ),
+        in_specs=[smem()] + [hbm() for _ in range(9)],
+        out_specs=(hbm(), hbm(), vmem(), vmem(), vmem()),
+        scratch_shapes=[
+            pltpu.SMEM(row_offset.shape, jnp.int32),
+            pltpu.SMEM(col_offset.shape, jnp.int32),
+            pltpu.VMEM(firsts, jnp.int32),
+            pltpu.VMEM(firsts, jnp.int32),
+            pltpu.VMEM(row_taps.shape, bf16),
+            pltpu.VMEM(col_taps.shape, bf16),
+            weights,
+            weights,
+            pltpu.SemaphoreType.DMA((9,)),
+            pltpu.SemaphoreType.DMA((2, NG)),
+        ],
         compiler_params=params,
         name="taps",
-    )(blocks_used, row_offset, col_offset, row_first, col_first, row_taps, col_taps)
+    )(
+        blocks_used,
+        *map(in_hbm, (row_offset, col_offset, row_first.reshape(firsts), col_first.reshape(firsts), row_taps, col_taps)),
+        *map(in_hbm, (forward, coil_maps, samples)),
+    )
 
     momentum = 1.0
     misfit = None
@@ -295,11 +353,13 @@
         gathered = exchanged(send)
         left, right = neighbours(moving)
         if step_num == 0:
-            gathered, left, right, wx, wy = lax.optimization_barrier((gathered, left, right, wx, wy))
+            gathered, left, right, wx, wy, forward, maps, measured = lax.optimization_barrier(
+                (gathered, left, right, wx, wy, forward, maps, measured)
+            )
         else:
             gathered, left, right = lax.optimization_barrier((gathered, left, right))
-        inputs = [blocks_used, gathered, coil_maps, samples, forward, adjoint, wx, wy]
-        specs = [smem(), vmem(), vmem(), vmem(), vmem(), vmem(), anywhere(), anywhere()]
+        inputs = [blocks_used, gathered, maps, measured, forward, in_hbm(wx), in_hbm(wy)]
+        specs = [smem(), vmem(), vmem(), vmem(), vmem(), hbm(), hbm()]
         if last:
             inputs.append(misfit)
             specs.append(vmem())
@@ -312,8 +372,8 @@
             in_specs=specs,
             out_specs=tuple(vmem() for _ in out_shape),
             scratch_shapes=[
-                pltpu.VMEM((NG, N, GS), bf16),
-                pltpu.VMEM((NG, N, GS), bf16),
+                weights,
+                weights,
                 pltpu.VMEM((2 * N, N), f32),
                 pltpu.SemaphoreType.DMA((2, NG)),
             ],
@@ -328,7 +388,7 @@
         carry_on = (momentum - 1.0) / following
         inputs = [parts, moving, left, right]
         if last:
-            out_shape = (shape(initial_image.shape, f32), shape((ITERS, 128), f32))
+            out_shape = (shape(initial_image.shape, f32), shape((1, ITERS), f32))
         else:
             inputs.append(current)
             out_shape = (send_shape, rows_shape, rows_shape)
@@ -345,7 +405,7 @@
         else:
             send, current, moving = results
         momentum = following
-    return image, misfit_rows[:, :1]
+    return image, misfit_rows.T
 
 
 def solution(mesh):

time: 106 us -> 92 us (0.87)
  the two profiles are of different devices: /device:TPU:64 before, /device:TPU:32 now
where the time goes in v2:
time: 92 us; the launch traced here: 92.2 us
  blocking collectives  34.6 us (38%)
  starting transfers between devices  20.5 us (22%)
  waiting for transfers between devices  19.9 us (22%)
  Pallas kernels  15.8 us (17%)
  between operations  1.36 us (1%)
    all_to_all x2, blocking collectives, exchanged(): return lax.all_to_all(parts, 'coil', 0, 0, tiled=True)  34.6 us
    all_to_all x2, starting transfers between devices, exchanged(): return lax.all_to_all(parts, 'coil', 0, 0, tiled=True)  19.5 us
    all_to_all x2, waiting for transfers between devices, exchanged(): return lax.all_to_all(parts, 'coil', 0, 0, tiled=True)  16 us
    pallas_call x2, Pallas kernels, on_device(): pl.pallas_call(lambda *refs, last=last: coil_kernel(last, *refs), out_sha...  9.17 us
    pallas_call x1, Pallas kernels, on_device(): pl.pallas_call(taps_kernel, out_shape=(pltpu.HBM((NG, N, GS), bf16), pltp...  3.47 us
    ppermute x2, waiting for transfers between devices, neighbours(): lax.ppermute(values, 'frame', [(i, (i + 1) % count) for i in range(count)])  2.95 us
  transfers between devices with their start and end apart: 6, of which 4 were waited for; matrix products, arithmetic and copies ran while one was open for 0% of the time, Pallas kernels for 4%

profile of v2, /device:TPU:32, one launch (start us, length us, event | category | flops | bytes accessed | tf_op | source)
XLA Modules:
  0.0 92.2 jit_solution(16363930217622502469)
XLA Ops:
  0.6 1.5 %start.1 = (bf16[32,8,512]{2,1,0:T(8,128)(2,1)}, f32[8,512]{1,0:T(8,128)S(1)}) custom-call(f32[8,1,2,256]{3,2,1,0:T(2,128)} %image_hbm.1), custom_call_target="tpu_custom_call" | custom-call | tf_op jit(solution)/shard_map/start/pallas_call | solution.py:305
  2.1 13.2 %all-to-all-start = ((bf16[32,8,512]{2,1,0:T(8,128)(2,1)}), bf16[32,8,512]{2,1,0:T(8,128)(2,1)S(1)}, u32[]{:S(2)}, u32[]{:S(2)}) async-start(bf16[32,8,512]{2,1,0:T(8,128)(2,1)} %get-tuple-element.26), calls=%async_computation | async-start | bytes 524288 | tf_op jit(solution)/shard_map/all_to_all | solution.py:274
  15.3 0.0 collective-permute-start.1
  15.3 0.5 collective-permute-start
  16.5 3.5 %taps.1 = (bf16[9,256,512]{2,1,0:T(8,128)(2,1)}, bf16[9,256,512]{2,1,0:T(8,128)(2,1)}, bf16[512,512]{1,0:T(8,128)(2,1)S(1)}, bf16[1,2,256,256]{3,2,1,0:T(8,128)(2,1)S(1)}, bf16[1,1,18,2,256]{4,3,2,1,0:T(2,128)(2,1)S(1)}) custom-call(s32[1]{0:T(128)S(6)} %copy.13.count_ref.refs_0_, s32[1,18]{1,0:T(1,128)} %refs_0_.3, s32[1,18]{1,0:T(1,128)} %refs_1_.1, ...), custom_call_target="tpu_custom_call" | custom-call | tf_op jit(solution)/shard_map/taps/pallas_call | solution.py:318
  20.0 0.0 collective-permute-done.1.refs_3_
  20.0 0.0 collective-permute-done.refs_2_
  20.0 7.8 %all-to-all-done.refs_1_ = bf16[32,8,512]{2,1,0:T(8,128)(2,1)S(1)} async-done(((bf16[32,8,512]{2,1,0:T(8,128)(2,1)}), bf16[32,8,512]{2,1,0:T(8,128)(2,1)S(1)}, u32[]{:S(2)}, u32[]{:S(2)}) %all-to-all-start) | async-done | bytes 262176 | tf_op jit(solution)/shard_map/all_to_all | solution.py:274
  27.7 4.6 %coil0.1 = (bf16[32,8,512]{2,1,0:T(8,128)(2,1)S(1)}, f32[8,128]{1,0:T(8,128)S(1)}) custom-call(s32[1]{0:T(128)S(6)} %copy.13.count_ref.refs_0_, bf16[32,8,512]{2,1,0:T(8,128)(2,1)S(1)} %all-to-all-done.refs_1_, bf16[1,2,256,256]{3,2,1,0:T(8,128)(2,1)S(1)} %get-tuple-element.34.refs_2_, bf16[1,1,18,2,256]{4,3,2,1,0:T(2,128)(2,1)S(1)} %get-tuple-element.35.refs_3_, ...), custom_call_target="tpu_custom_call" | custom-call | tf_op jit(solution)/shard_map/coil0/pallas_call | solution.py:369
  32.3 15.9 %all_to_all.20.refs_0_ = bf16[32,8,512]{2,1,0:T(8,128)(2,1)S(1)} all-to-all(bf16[32,8,512]{2,1,0:T(8,128)(2,1)S(1)} %get-tuple-element.39), channel_id=1, replica_groups=mesh['coil'=32,'frame'=16] {'coil'}, dimensions={0} | all-to-all | bytes 524288 | tf_op jit(solution)/shard_map/all_to_all | solution.py:274
  48.3 0.9 %update0.1 = (bf16[32,8,512]{2,1,0:T(8,128)(2,1)}, f32[8,512]{1,0:T(8,128)}, f32[8,512]{1,0:T(8,128)S(1)}) custom-call(bf16[32,8,512]{2,1,0:T(8,128)(2,1)S(1)} %all_to_all.20.refs_0_, f32[8,512]{1,0:T(8,128)S(1)} %get-tuple-element.27.refs_1_.refs_4_, f32[8,512]{1,0:T(8,128)S(1)} %collective-permute-done.refs_2_, ...), custom_call_target="tpu_custom_call" | custom-call | tf_op jit(solution)/shard_map/update0/pallas_call | solution.py:395
  49.2 6.3 %all-to-all-start.2 = ((bf16[32,8,512]{2,1,0:T(8,128)(2,1)}), bf16[32,8,512]{2,1,0:T(8,128)(2,1)S(1)}, u32[]{:S(2)}, u32[]{:S(2)}) async-start(bf16[32,8,512]{2,1,0:T(8,128)(2,1)} %get-tuple-element.42), calls=%async_computation.2 | async-start | bytes 524288 | tf_op jit(solution)/shard_map/all_to_all | solution.py:274
  55.5 0.0 collective-permute-start.3
  55.6 0.5 collective-permute-start.2
  56.1 0.9 %collective-permute-done.3.refs_3_ = f32[8,512]{1,0:T(8,128)S(1)} collective-permute-done((f32[8,512]{1,0:T(8,128)S(1)}, f32[8,512]{1,0:T(8,128)S(1)}, u32[]{:S(2)}, u32[]{:S(2)}) %collective-permute-start.3) | collective-permute-done | bytes 16416 | tf_op jit(solution)/shard_map/ppermute | solution.py:280
  57.0 3.0 %collective-permute-done.2.refs_2_ = f32[8,512]{1,0:T(8,128)S(1)} collective-permute-done((f32[8,512]{1,0:T(8,128)S(1)}, f32[8,512]{1,0:T(8,128)S(1)}, u32[]{:S(2)}, u32[]{:S(2)}) %collective-permute-start.2) | collective-permute-done | bytes 16416 | tf_op jit(solution)/shard_map/ppermute | solution.py:279
  59.9 8.2 %all-to-all-done.2.refs_1_ = bf16[32,8,512]{2,1,0:T(8,128)(2,1)S(1)} async-done(((bf16[32,8,512]{2,1,0:T(8,128)(2,1)}), bf16[32,8,512]{2,1,0:T(8,128)(2,1)S(1)}, u32[]{:S(2)}, u32[]{:S(2)}) %all-to-all-start.2) | async-done | bytes 262176 | tf_op jit(solution)/shard_map/all_to_all | solution.py:274
  68.2 4.6 %coil1.1 = bf16[32,8,640]{2,1,0:T(8,128)(2,1)S(1)} custom-call(s32[1]{0:T(128)S(6)} %copy.13.count_ref.refs_0_, bf16[32,8,512]{2,1,0:T(8,128)(2,1)S(1)} %all-to-all-done.2.refs_1_, bf16[1,2,256,256]{3,2,1,0:T(8,128)(2,1)S(1)} %get-tuple-element.34.refs_2_, bf16[1,1,18,2,256]{4,3,2,1,0:T(2,128)(2,1)S(1)} %get-tuple-element.35.refs_3_, ...), custom_call_target="tpu_custom_call" | custom-call | tf_op jit(solution)/shard_map/coil1/pallas_call | solution.py:369
  72.8 18.6 %all_to_all.21.refs_0_ = bf16[32,8,640]{2,1,0:T(8,128)(2,1)S(1)} all-to-all(bf16[32,8,640]{2,1,0:T(8,128)(2,1)S(1)} %coil1.1), channel_id=1, replica_groups=mesh['coil'=32,'frame'=16] {'coil'}, dimensions={0} | all-to-all | bytes 655360 | tf_op jit(solution)/shard_map/all_to_all | solution.py:274
  91.4 0.8 update1.1
Async XLA Ops:
  2.1 25.6 %all-to-all-start = ((bf16[32,8,512]{2,1,0:T(8,128)(2,1)}), bf16[32,8,512]{2,1,0:T(8,128)(2,1)S(1)}, u32[]{:S(2)}, u32[]{:S(2)}) async-start(bf16[32,8,512]{2,1,0:T(8,128)(2,1)} %get-tuple-element.26), calls=%async_computation | async-start | bytes 524288 | tf_op jit(solution)/shard_map/all_to_all | solution.py:274
  15.3 4.7 %collective-permute-start.1 = (f32[8,512]{1,0:T(8,128)S(1)}, f32[8,512]{1,0:T(8,128)S(1)}, u32[]{:S(2)}, u32[]{:S(2)}) collective-permute-start(f32[8,512]{1,0:T(8,128)S(1)} %get-tuple-element.27.refs_1_.refs_4_), channel_id=1, source_target_pairs={{1,0},{2,1},{3,2},{4,3},{5,4},{6,5},{7,6},{8,7},{9,8},{10,9},{11,1... | collective-permute-start | bytes 49160 | tf_op jit(solution)/shard_map/ppermute | solution.py:280
  15.3 4.6 %collective-permute-start = (f32[8,512]{1,0:T(8,128)S(1)}, f32[8,512]{1,0:T(8,128)S(1)}, u32[]{:S(2)}, u32[]{:S(2)}) collective-permute-start(f32[8,512]{1,0:T(8,128)S(1)} %get-tuple-element.27.refs_1_.refs_4_), channel_id=1, source_target_pairs={{0,1},{1,2},{2,3},{3,4},{4,5},{5,6},{6,7},{7,8},{8,9},{9,10},{10,1... | collective-permute-start | bytes 49160 | tf_op jit(solution)/shard_map/ppermute | solution.py:279
  49.2 19.0 %all-to-all-start.2 = ((bf16[32,8,512]{2,1,0:T(8,128)(2,1)}), bf16[32,8,512]{2,1,0:T(8,128)(2,1)S(1)}, u32[]{:S(2)}, u32[]{:S(2)}) async-start(bf16[32,8,512]{2,1,0:T(8,128)(2,1)} %get-tuple-element.42), calls=%async_computation.2 | async-start | bytes 524288 | tf_op jit(solution)/shard_map/all_to_all | solution.py:274
  55.5 1.5 %collective-permute-start.3 = (f32[8,512]{1,0:T(8,128)S(1)}, f32[8,512]{1,0:T(8,128)S(1)}, u32[]{:S(2)}, u32[]{:S(2)}) collective-permute-start(f32[8,512]{1,0:T(8,128)S(1)} %get-tuple-element.43.refs_1_), channel_id=1, source_target_pairs={{1,0},{2,1},{3,2},{4,3},{5,4},{6,5},{7,6},{8,7},{9,8},{10,9},{11,1... | collective-permute-start | bytes 49160 | tf_op jit(solution)/shard_map/ppermute | solution.py:280
  55.6 4.4 %collective-permute-start.2 = (f32[8,512]{1,0:T(8,128)S(1)}, f32[8,512]{1,0:T(8,128)S(1)}, u32[]{:S(2)}, u32[]{:S(2)}) collective-permute-start(f32[8,512]{1,0:T(8,128)S(1)} %get-tuple-element.43.refs_1_), channel_id=1, source_target_pairs={{0,1},{1,2},{2,3},{3,4},{4,5},{5,6},{6,7},{7,8},{8,9},{9,10},{10,1... | collective-permute-start | bytes 49160 | tf_op jit(solution)/shard_map/ppermute | solution.py:279

commit v3 on v2

--- a/solution.py
+++ b/solution.py
@@ -13,9 +13,11 @@
 BS = 256
 KW = 4
 ITERS = 2
-GROUP = 2
+TT = 128
+GROUP = 6
 NG = NB // GROUP
-GS = GROUP * BS
+ALIGN = 16
+WINDOW = TT + ALIGN
 
 step_size = 2.0
 tv_weight = 0.1
@@ -71,51 +73,60 @@
     send_ref[...] = jnp.broadcast_to(low[None], send_ref.shape)
 
 
-def taps_kernel(count_ref, *refs):
-    sources, (wx_hbm, wy_hbm), kept, held = refs[:9], refs[9:11], refs[11:14], refs[14:20]
-    wx_ref, wy_ref, in_sems, out_sems = refs[20:]
-    row_off, col_off, row_first, col_first, row_taps, col_taps = held
+def window_start(offset):
+    return pl.multiple_of(jnp.minimum((offset >> 4) << 4, N - WINDOW), ALIGN)
+
+
+def taps_kernel(count_ref, row_off, col_off, *refs):
+    sources, (wx_hbm, wy_hbm, wx_keep, wy_keep), kept, held = refs[:7], refs[7:11], refs[11:14], refs[14:18]
+    wx_ref, wy_ref, in_sems, out_sems = refs[18:]
+    row_first, col_first, row_taps, col_taps = held
     loads = [pltpu.make_async_copy(source, own, in_sems.at[k]) for k, (source, own) in enumerate(zip(sources, held + kept))]
     for load in loads:
         load.start()
     for load in loads[: len(held)]:
         load.wait()
     groups = (count_ref[0] + GROUP - 1) // GROUP
-    position = lax.broadcasted_iota(jnp.int32, (N, BS), 0)
 
     def stores(group):
+        blocks = pl.ds(group * GROUP - GROUP, GROUP)
         return (
-            pltpu.make_async_copy(wx_ref.at[group], wx_hbm.at[group], out_sems.at[0, group]),
-            pltpu.make_async_copy(wy_ref.at[group], wy_hbm.at[group], out_sems.at[1, group]),
+            pltpu.make_async_copy(wx_ref.at[blocks], wx_hbm.at[blocks], out_sems.at[0, group]),
+            pltpu.make_async_copy(wy_ref.at[blocks], wy_hbm.at[blocks], out_sems.at[1, group]),
         )
 
-    def build(start, taps):
-        offset = position - start
-        matrix = jnp.zeros((N, BS), f32)
+    def matrix(length, start, taps):
+        offset = lax.broadcasted_iota(jnp.int32, (length, BS), 0) - start
+        values = jnp.zeros((length, BS), f32)
         for tap in range(KW):
-            matrix = jnp.where(offset == tap, taps[tap : tap + 1], matrix)
-        return matrix.astype(bf16)
+            values = jnp.where(offset == tap, taps[tap : tap + 1], values)
+        return values.astype(bf16)
+
+    def build(block, wx_out, wy_out, place):
+        col = col_off[block]
+        wx_out[place] = matrix(N, row_first[block] + row_off[block], row_taps[0, block].astype(f32))
+        wy_out[place] = matrix(WINDOW, col_first[block] + (col - window_start(col)), col_taps[0, block].astype(f32))
+
+    def first(block, carry):
+        build(block, wx_keep, wy_keep, block)
+        return carry
 
     def visit(group, carry):
         for member in range(GROUP):
             block = group * GROUP + member
-            lanes = slice(member * BS, (member + 1) * BS)
-            row_start = row_first[block] + row_off[0, block]
-            col_start = col_first[block] + col_off[0, block]
-            wx_ref[group, :, lanes] = build(row_start, row_taps[0, block].astype(f32))
-            wy_ref[group, :, lanes] = build(col_start, col_taps[0, block].astype(f32))
+            build(block, wx_ref, wy_ref, block - GROUP)
         for store in stores(group):
             store.start()
         return carry
-
-    lax.fori_loop(0, groups, visit, 0)
 
     def finish(group, carry):
         for store in stores(group):
             store.wait()
         return carry
 
-    lax.fori_loop(0, groups, finish, 0)
+    lax.fori_loop(1, groups, visit, 0)
+    lax.fori_loop(0, GROUP, first, 0)
+    lax.fori_loop(1, groups, finish, 0)
     for load in loads[len(held) :]:
         load.wait()
 
@@ -129,19 +140,20 @@
 
 
 def coil_kernel(last, *refs):
+    (count_ref, col_off, image_ref, maps_ref, samples_ref, fwd_ref, wx_keep, wy_keep, wx_hbm, wy_hbm) = refs[:10]
     if last:
-        (count_ref, image_ref, maps_ref, samples_ref, fwd_ref, wx_hbm, wy_hbm, before_ref) = refs[:8]
-        (send_ref, wx_ref, wy_ref, grid_ref, sems) = refs[8:]
+        (before_ref, send_ref) = refs[10:12]
     else:
-        (count_ref, image_ref, maps_ref, samples_ref, fwd_ref, wx_hbm, wy_hbm) = refs[:7]
-        (send_ref, misfit_ref, wx_ref, wy_ref, grid_ref, sems) = refs[7:]
+        (send_ref, misfit_ref) = refs[10:12]
+    (wx_ref, wy_ref, kspace_ref, grid_ref, sems) = refs[12:]
     count = count_ref[0]
     groups = (count + GROUP - 1) // GROUP
 
     def copies(group):
+        blocks = pl.ds(group * GROUP - GROUP, GROUP)
         return (
-            pltpu.make_async_copy(wx_hbm.at[group], wx_ref.at[group], sems.at[0, group]),
-            pltpu.make_async_copy(wy_hbm.at[group], wy_ref.at[group], sems.at[1, group]),
+            pltpu.make_async_copy(wx_hbm.at[blocks], wx_ref.at[blocks], sems.at[0, group]),
+            pltpu.make_async_copy(wy_hbm.at[blocks], wy_ref.at[blocks], sems.at[1, group]),
         )
 
     def fetch(group, carry):
@@ -149,7 +161,7 @@
             copy.start()
         return carry
 
-    lax.fori_loop(0, groups, fetch, 0)
+    lax.fori_loop(1, groups, fetch, 0)
 
     image = image_ref[...].astype(f32)
     real = image[:, :, :N].reshape(N, N)
@@ -159,43 +171,54 @@
     coil_real = (map_real * real - map_imag * imag).astype(bf16)
     coil_imag = (map_real * imag + map_imag * real).astype(bf16)
     coil_image = jnp.concatenate([coil_real, coil_imag], axis=0)
-    half = dot(fwd_ref[...], coil_image).astype(bf16)
-    half = jnp.concatenate([half[:N], half[N:]], axis=1)
-    kspace = dot_nt(fwd_ref[...], half).astype(bf16)
+    half = [dot(fwd_ref[part * N : (part + 1) * N], coil_image).astype(bf16) for part in range(2)]
+    half = jnp.concatenate(half, axis=1)
+    for part in range(2):
+        kspace_ref[part] = dot_nt(fwd_ref[part * N : (part + 1) * N], half).astype(bf16)
     grid_ref[...] = jnp.zeros_like(grid_ref)
 
-    def visit(group, misfit):
+    def visit(group, wx_in, wy_in, misfit):
+        for member in range(GROUP):
+            block = group * GROUP + member
+            place = member if wx_in is wx_keep else block - GROUP
+            window = pl.ds(window_start(col_off[block]), WINDOW)
+            wx = wx_in[place]
+            wy = wy_in[place]
+            wy_wide = wy.astype(f32)
+            measured = samples_ref[0, 0, block].astype(f32)
+            tile = jnp.concatenate([kspace_ref[0, window, :], kspace_ref[1, window, :]], axis=0)
+            across = dot(tile, wx)
+            weighted = []
+            for part in range(2):
+                predicted = jnp.sum(across[part * WINDOW : (part + 1) * WINDOW] * wy_wide, axis=0, keepdims=True)
+                resid = jnp.where(block < count, predicted - measured[part : part + 1], 0.0)
+                misfit = misfit + resid * resid
+                weighted.append(wy * resid.astype(bf16))
+            spread = dot_nt(jnp.concatenate(weighted, axis=0), wx)
+            for part in range(2):
+                grid_ref[part, window, :] += spread[part * WINDOW : (part + 1) * WINDOW]
+        return misfit
+
+    def later(group, misfit):
         for copy in copies(group):
             copy.wait()
-        wx = wx_ref[group]
-        wy = wy_ref[group]
-        wy_wide = wy.astype(f32)
-        across = dot(kspace, wx)
-        weighted = []
-        for part in range(2):
-            predicted = jnp.sum(across[part * N : (part + 1) * N] * wy_wide, axis=0, keepdims=True)
-            resid = []
-            for member in range(GROUP):
-                block = group * GROUP + member
-                measured = samples_ref[0, 0, block].astype(f32)[part : part + 1]
-                off = predicted[:, member * BS : (member + 1) * BS] - measured
-                resid.append(jnp.where(block < count, off, 0.0))
-            resid = jnp.concatenate(resid, axis=1)
-            misfit = misfit + resid * resid
-            weighted.append(wy * resid.astype(bf16))
-        weighted = jnp.concatenate(weighted, axis=0)
-        grid_ref[...] += dot_nt(weighted, wx)
-        return misfit
-
-    misfit = lax.fori_loop(0, groups, visit, jnp.zeros((1, GS), f32))
+        return visit(group, wx_ref, wy_ref, misfit)
+
+    misfit = visit(0, wx_keep, wy_keep, jnp.zeros((1, BS), f32))
+    misfit = lax.fori_loop(1, groups, later, misfit)
     misfit = jnp.broadcast_to(jnp.sum(misfit, axis=1, keepdims=True), (8, 128))
 
-    grid = jnp.concatenate([grid_ref[:N].astype(bf16), -grid_ref[N:].astype(bf16)], axis=1)
-    back_half = dot_nt(fwd_ref[...], grid)
-    back_half = jnp.concatenate([back_half[:N].astype(bf16), -back_half[N:].astype(bf16)], axis=1)
+    grid_real = grid_ref[0].astype(bf16)
+    grid_imag = grid_ref[1].astype(bf16)
+    grid = jnp.concatenate([grid_real, -grid_imag], axis=1)
+    back_real = dot_nt(fwd_ref[:N], grid).astype(bf16)
+    back_imag = dot_nt(fwd_ref[N:], grid).astype(bf16)
+    back_half = jnp.concatenate([back_real, -back_imag], axis=1)
     back = dot(back_half, fwd_ref[...])
     back_real = back[:, :N]
     back_imag = back[:, N:]
+    map_real = maps_ref[0, 0].astype(f32)
+    map_imag = maps_ref[0, 1].astype(f32)
     out_real = map_real * back_real + map_imag * back_imag
     out_imag = map_real * back_imag - map_imag * back_real
     parts = send_ref.shape[0]
@@ -230,7 +253,7 @@
     if last:
         (parts_ref, moving_ref, left_ref, right_ref, image_ref, misfit_ref) = refs
     else:
-        (parts_ref, moving_ref, left_ref, right_ref, current_ref, send_ref, updated_ref, next_ref) = refs
+        (parts_ref, moving_ref, left_ref, right_ref, current_ref, send_ref, next_ref) = refs
     total = jnp.sum(parts_ref[...].astype(f32), axis=0)
     moving = moving_ref[...]
     tv_grad = unit_change(moving - left_ref[...]) - unit_change(right_ref[...] - moving)
@@ -265,7 +288,6 @@
         misfit_ref[...] = jnp.where(lane == 0, first, second)[:, :ITERS]
     else:
         following = updated + carry_on * (updated - current_ref[...])
-        updated_ref[...] = updated
         next_ref[...] = following
         send_ref[...] = jnp.broadcast_to(following.astype(bf16)[None], send_ref.shape)
 
@@ -299,8 +321,8 @@
     forward = pair_table(N)
     params = pltpu.CompilerParams(vmem_limit_bytes=32 * 1024 * 1024)
     shape = jax.ShapeDtypeStruct
-    send_shape = shape((coils, rows, 2 * N), bf16)
-    rows_shape = shape((rows, 2 * N), f32)
+    send_shape = pltpu.VMEM((coils, rows, 2 * N), bf16)
+    rows_shape = pltpu.VMEM((rows, 2 * N), f32)
 
     send, moving = pl.pallas_call(
         start_kernel,
@@ -311,38 +333,43 @@
         compiler_params=params,
         name="start",
     )(in_hbm(initial_image))
-    current = moving
+    initial = moving
 
     firsts = (NB, 1, BS)
-    weights = pltpu.VMEM((NG, N, GS), bf16)
-    wx, wy, forward, maps, measured = pl.pallas_call(
+    wx_shape = (NB - GROUP, N, BS)
+    wy_shape = (NB - GROUP, WINDOW, BS)
+    row_off = row_offset.reshape(NB)
+    col_off = col_offset.reshape(NB)
+    constants = pl.pallas_call(
         taps_kernel,
         out_shape=(
-            pltpu.HBM((NG, N, GS), bf16),
-            pltpu.HBM((NG, N, GS), bf16),
+            pltpu.HBM(wx_shape, bf16),
+            pltpu.HBM(wy_shape, bf16),
+            pltpu.VMEM((GROUP, N, BS), bf16),
+            pltpu.VMEM((GROUP, WINDOW, BS), bf16),
             pltpu.VMEM(forward.shape, bf16),
             pltpu.VMEM(coil_maps.shape, bf16),
             pltpu.VMEM(samples.shape, bf16),
         ),
-        in_specs=[smem()] + [hbm() for _ in range(9)],
-        out_specs=(hbm(), hbm(), vmem(), vmem(), vmem()),
+        in_specs=[smem(), smem(), smem()] + [hbm() for _ in range(7)],
+        out_specs=(hbm(), hbm(), vmem(), vmem(), vmem(), vmem(), vmem()),
         scratch_shapes=[
-            pltpu.SMEM(row_offset.shape, jnp.int32),
-            pltpu.SMEM(col_offset.shape, jnp.int32),
             pltpu.VMEM(firsts, jnp.int32),
             pltpu.VMEM(firsts, jnp.int32),
             pltpu.VMEM(row_taps.shape, bf16),
             pltpu.VMEM(col_taps.shape, bf16),
-            weights,
-            weights,
-            pltpu.SemaphoreType.DMA((9,)),
+            pltpu.VMEM(wx_shape, bf16),
+            pltpu.VMEM(wy_shape, bf16),
+            pltpu.SemaphoreType.DMA((7,)),
             pltpu.SemaphoreType.DMA((2, NG)),
         ],
         compiler_params=params,
         name="taps",
     )(
         blocks_used,
-        *map(in_hbm, (row_offset, col_offset, row_first.reshape(firsts), col_first.reshape(firsts), row_taps, col_taps)),
+        row_off,
+        col_off,
+        *map(in_hbm, (row_first.reshape(firsts), col_first.reshape(firsts), row_taps, col_taps)),
         *map(in_hbm, (forward, coil_maps, samples)),
     )
 
@@ -353,17 +380,16 @@
         gathered = exchanged(send)
         left, right = neighbours(moving)
         if step_num == 0:
-            gathered, left, right, wx, wy, forward, maps, measured = lax.optimization_barrier(
-                (gathered, left, right, wx, wy, forward, maps, measured)
-            )
+            gathered, left, right, constants = lax.optimization_barrier((gathered, left, right, constants))
+            wx, wy, wx_keep, wy_keep, forward, maps, measured = constants
         else:
             gathered, left, right = lax.optimization_barrier((gathered, left, right))
-        inputs = [blocks_used, gathered, maps, measured, forward, in_hbm(wx), in_hbm(wy)]
-        specs = [smem(), vmem(), vmem(), vmem(), vmem(), hbm(), hbm()]
+        inputs = [blocks_used, col_off, gathered, maps, measured, forward, wx_keep, wy_keep, in_hbm(wx), in_hbm(wy)]
+        specs = [smem(), smem()] + [vmem() for _ in range(6)] + [hbm(), hbm()]
         if last:
             inputs.append(misfit)
             specs.append(vmem())
-            out_shape = (shape((coils, rows, 2 * N + 128), bf16),)
+            out_shape = (pltpu.VMEM((coils, rows, 2 * N + 128), bf16),)
         else:
             out_shape = (send_shape, shape((8, 128), f32))
         results = pl.pallas_call(
@@ -372,9 +398,10 @@
             in_specs=specs,
             out_specs=tuple(vmem() for _ in out_shape),
             scratch_shapes=[
-                weights,
-                weights,
-                pltpu.VMEM((2 * N, N), f32),
+                pltpu.VMEM(wx_shape, bf16),
+                pltpu.VMEM(wy_shape, bf16),
+                pltpu.VMEM((2, N, N), bf16),
+                pltpu.VMEM((2, N, N), f32),
                 pltpu.SemaphoreType.DMA((2, NG)),
             ],
             compiler_params=params,
@@ -390,8 +417,8 @@
         if last:
             out_shape = (shape(initial_image.shape, f32), shape((1, ITERS), f32))
         else:
-            inputs.append(current)
-            out_shape = (send_shape, rows_shape, rows_shape)
+            inputs.append(initial)
+            out_shape = (send_shape, rows_shape)
         results = pl.pallas_call(
             lambda *refs, last=last, carry_on=carry_on: update_kernel(last, carry_on, misfit_scale, *refs),
             out_shape=out_shape,
@@ -403,7 +430,7 @@
         if last:
             image, misfit_rows = results
         else:
-            send, current, moving = results
+            send, moving = results
         momentum = following
     return image, misfit_rows.T
 

time: 92 us -> 88.8 us (0.965)
  the two profiles are of different devices: /device:TPU:32 before, /device:TPU:57 now
where the time goes in v3:
time: 88.8 us; the launch traced here: 88.3 us
  blocking collectives  37.9 us (43%)
  starting transfers between devices  23 us (26%)
  Pallas kernels  15.5 us (17%)
  waiting for transfers between devices  9.23 us (10%)
  between operations  1.37 us (2%)
  local copies, waits for them, and re-layouts  1.31 us (1%)
    all_to_all x2, blocking collectives, exchanged(): return lax.all_to_all(parts, 'coil', 0, 0, tiled=True)  37.9 us
    all_to_all x2, starting transfers between devices, exchanged(): return lax.all_to_all(parts, 'coil', 0, 0, tiled=True)  17 us
    pallas_call x2, Pallas kernels, on_device(): pl.pallas_call(lambda *refs, last=last: coil_kernel(last, *refs), out_sha...  8.44 us
    all_to_all x2, waiting for transfers between devices, exchanged(): return lax.all_to_all(parts, 'coil', 0, 0, tiled=True)  7.51 us
    ppermute x2, starting transfers between devices, neighbours(): lax.ppermute(values, 'frame', [(i, (i + 1) % count) for i in range(count)])  4.94 us
    pallas_call x1, Pallas kernels, on_device(): pl.pallas_call(taps_kernel, out_shape=(pltpu.HBM(wx_shape, bf16), pltpu.H...  3.92 us
  transfers between devices with their start and end apart: 6, of which 3 were waited for; matrix products, arithmetic and copies ran while one was open for 0% of the time, Pallas kernels for 4%

profile of v3, /device:TPU:57, one launch (start us, length us, event | category | flops | bytes accessed | tf_op | source)
XLA Modules:
  0.0 88.3 jit_solution(2580886682466022123)
XLA Ops:
  0.6 1.5 %start.1 = (bf16[32,8,512]{2,1,0:T(8,128)(2,1)}, f32[8,512]{1,0:T(8,128)S(1)}) custom-call(f32[8,1,2,256]{3,2,1,0:T(2,128)} %image_hbm.1), custom_call_target="tpu_custom_call" | custom-call | tf_op jit(solution)/shard_map/start/pallas_call | solution.py:327
  2.1 12.9 %all-to-all-start = ((bf16[32,8,512]{2,1,0:T(8,128)(2,1)}), bf16[32,8,512]{2,1,0:T(8,128)(2,1)S(1)}, u32[]{:S(2)}, u32[]{:S(2)}) async-start(bf16[32,8,512]{2,1,0:T(8,128)(2,1)} %get-tuple-element.30), calls=%async_computation | async-start | bytes 524288 | tf_op jit(solution)/shard_map/all_to_all | solution.py:296
  15.0 1.0 %collective-permute-start.1 = (f32[8,512]{1,0:T(8,128)S(1)}, f32[8,512]{1,0:T(8,128)S(1)}, u32[]{:S(2)}, u32[]{:S(2)}) collective-permute-start(f32[8,512]{1,0:T(8,128)S(1)} %get-tuple-element.31.refs_1_.refs_4_), channel_id=1, source_target_pairs={{1,0},{2,1},{3,2},{4,3},{5,4},{6,5},{7,6},{8,7},{9,8},{10,9},{11,1... | collective-permute-start | bytes 49160 | tf_op jit(solution)/shard_map/ppermute | solution.py:302
  16.0 2.0 %collective-permute-start = (f32[8,512]{1,0:T(8,128)S(1)}, f32[8,512]{1,0:T(8,128)S(1)}, u32[]{:S(2)}, u32[]{:S(2)}) collective-permute-start(f32[8,512]{1,0:T(8,128)S(1)} %get-tuple-element.31.refs_1_.refs_4_), channel_id=1, source_target_pairs={{0,1},{1,2},{2,3},{3,4},{4,5},{5,6},{6,7},{7,8},{8,9},{9,10},{10,1... | collective-permute-start | bytes 49160 | tf_op jit(solution)/shard_map/ppermute | solution.py:301
  18.6 0.0 copy-start
  18.6 0.6 copy-done
  19.3 0.0 copy-start.2
  19.3 0.7 copy-done.2
  19.9 3.9 %taps.1 = (bf16[12,256,256]{2,1,0:T(8,128)(2,1)}, bf16[12,144,256]{2,1,0:T(8,128)(2,1)}, bf16[6,256,256]{2,1,0:T(8,128)(2,1)S(1)}, bf16[6,144,256]{2,1,0:T(8,128...) custom-call(s32[1]{0:T(128)S(6)} %copy.13.count_ref.refs_0_, ...), custom_call_target="tpu_custom_call" | custom-call | tf_op jit(solution)/shard_map/taps/pallas_call | solution.py:343
  23.9 0.0 collective-permute-done.1.refs_3_
  23.9 0.0 collective-permute-done.refs_2_
  23.9 0.8 all-to-all-done.refs_2_
  24.7 0.0 copy-start.1
  24.7 4.2 %coil0.1 = (bf16[32,8,512]{2,1,0:T(8,128)(2,1)S(1)}, f32[8,128]{1,0:T(8,128)S(1)}) custom-call(s32[1]{0:T(128)S(6)} %copy.13.count_ref.refs_0_, s32[18]{0:T(128)S(1)} %bitcast.6, bf16[32,8,512]{2,1,0:T(8,128)(2,1)S(1)} %all-to-all-done.refs_2_, bf16[1,2,256,256]{3,2,1,0:T(8,128)(2,1)S(1)} %get-tuple-element.40.refs_3_, ...), custom_call_target="tpu_custom_call" | custom-call | tf_op jit(solution)/shard_map/coil0/pallas_call | solution.py:395
  28.9 19.5 %all_to_all.20.refs_0_ = bf16[32,8,512]{2,1,0:T(8,128)(2,1)S(1)} all-to-all(bf16[32,8,512]{2,1,0:T(8,128)(2,1)S(1)} %get-tuple-element.47), channel_id=1, replica_groups=mesh['coil'=32,'frame'=16] {'coil'}, dimensions={0} | all-to-all | bytes 524288 | tf_op jit(solution)/shard_map/all_to_all | solution.py:296
  48.4 0.9 %update0.1 = (bf16[32,8,512]{2,1,0:T(8,128)(2,1)}, f32[8,512]{1,0:T(8,128)S(1)}) custom-call(bf16[32,8,512]{2,1,0:T(8,128)(2,1)S(1)} %all_to_all.20.refs_0_, f32[8,512]{1,0:T(8,128)S(1)} %get-tuple-element.31.refs_1_.refs_4_, f32[8,512]{1,0:T(8,128)S(1)} %collective-permute-done.refs_2_, f32[8,512]{1,0:T(8,128)S(1)} %collective-permute-done.1.refs_3_, ...), custom_call_target="tpu_custom_call" | custom-call | tf_op jit(solution)/shard_map/update0/pallas_call | solution.py:422
  49.3 4.1 %all-to-all-start.2 = ((bf16[32,8,512]{2,1,0:T(8,128)(2,1)}), bf16[32,8,512]{2,1,0:T(8,128)(2,1)S(1)}, u32[]{:S(2)}, u32[]{:S(2)}) async-start(bf16[32,8,512]{2,1,0:T(8,128)(2,1)} %get-tuple-element.50), calls=%async_computation.2 | async-start | bytes 524288 | tf_op jit(solution)/shard_map/all_to_all | solution.py:296
  53.4 0.0 collective-permute-start.3
  53.5 2.9 %collective-permute-start.2 = (f32[8,512]{1,0:T(8,128)S(1)}, f32[8,512]{1,0:T(8,128)S(1)}, u32[]{:S(2)}, u32[]{:S(2)}) collective-permute-start(f32[8,512]{1,0:T(8,128)S(1)} %get-tuple-element.51.refs_1_), channel_id=1, source_target_pairs={{0,1},{1,2},{2,3},{3,4},{4,5},{5,6},{6,7},{7,8},{8,9},{9,10},{10,1... | collective-permute-start | bytes 49160 | tf_op jit(solution)/shard_map/ppermute | solution.py:301
  56.4 1.7 %collective-permute-done.3.refs_3_ = f32[8,512]{1,0:T(8,128)S(1)} collective-permute-done((f32[8,512]{1,0:T(8,128)S(1)}, f32[8,512]{1,0:T(8,128)S(1)}, u32[]{:S(2)}, u32[]{:S(2)}) %collective-permute-start.3) | collective-permute-done | bytes 16416 | tf_op jit(solution)/shard_map/ppermute | solution.py:302
  58.1 0.0 collective-permute-done.2.refs_2_
  58.1 6.7 %all-to-all-done.2.refs_2_ = bf16[32,8,512]{2,1,0:T(8,128)(2,1)S(1)} async-done(((bf16[32,8,512]{2,1,0:T(8,128)(2,1)}), bf16[32,8,512]{2,1,0:T(8,128)(2,1)S(1)}, u32[]{:S(2)}, u32[]{:S(2)}) %all-to-all-start.2) | async-done | bytes 262176 | tf_op jit(solution)/shard_map/all_to_all | solution.py:296
  64.8 0.0 copy-done.1
  64.8 4.2 %coil1.1 = bf16[32,8,640]{2,1,0:T(8,128)(2,1)S(1)} custom-call(s32[1]{0:T(128)S(6)} %copy.13.count_ref.refs_0_, s32[18]{0:T(128)S(1)} %bitcast.7, bf16[32,8,512]{2,1,0:T(8,128)(2,1)S(1)} %all-to-all-done.2.refs_2_, bf16[1,2,256,256]{3,2,1,0:T(8,128)(2,1)S(1)} %get-tuple-element.40.refs_3_, bf16[1,1,18,2,256]{4,3,2,1,0:T(2,128)(2,1)S(1)} %get-tuple-element.41.refs_4_, ...), custom_call_target="tpu_custom_call" | custom-call | tf_op jit(solution)/shard_map/coil1/pallas_call | solution.py:395
  69.1 18.5 %all_to_all.21.refs_0_ = bf16[32,8,640]{2,1,0:T(8,128)(2,1)S(1)} all-to-all(bf16[32,8,640]{2,1,0:T(8,128)(2,1)S(1)} %coil1.1), channel_id=1, replica_groups=mesh['coil'=32,'frame'=16] {'coil'}, dimensions={0} | all-to-all | bytes 655360 | tf_op jit(solution)/shard_map/all_to_all | solution.py:296
  87.5 0.8 update1.1
Async XLA Ops:
  2.1 22.6 %all-to-all-start = ((bf16[32,8,512]{2,1,0:T(8,128)(2,1)}), bf16[32,8,512]{2,1,0:T(8,128)(2,1)S(1)}, u32[]{:S(2)}, u32[]{:S(2)}) async-start(bf16[32,8,512]{2,1,0:T(8,128)(2,1)} %get-tuple-element.30), calls=%async_computation | async-start | bytes 524288 | tf_op jit(solution)/shard_map/all_to_all | solution.py:296
  15.0 8.9 %collective-permute-start.1 = (f32[8,512]{1,0:T(8,128)S(1)}, f32[8,512]{1,0:T(8,128)S(1)}, u32[]{:S(2)}, u32[]{:S(2)}) collective-permute-start(f32[8,512]{1,0:T(8,128)S(1)} %get-tuple-element.31.refs_1_.refs_4_), channel_id=1, source_target_pairs={{1,0},{2,1},{3,2},{4,3},{5,4},{6,5},{7,6},{8,7},{9,8},{10,9},{11,1... | collective-permute-start | bytes 49160 | tf_op jit(solution)/shard_map/ppermute | solution.py:302
  16.0 7.9 %collective-permute-start = (f32[8,512]{1,0:T(8,128)S(1)}, f32[8,512]{1,0:T(8,128)S(1)}, u32[]{:S(2)}, u32[]{:S(2)}) collective-permute-start(f32[8,512]{1,0:T(8,128)S(1)} %get-tuple-element.31.refs_1_.refs_4_), channel_id=1, source_target_pairs={{0,1},{1,2},{2,3},{3,4},{4,5},{5,6},{6,7},{7,8},{8,9},{9,10},{10,1... | collective-permute-start | bytes 49160 | tf_op jit(solution)/shard_map/ppermute | solution.py:301
  18.6 0.7 copy-start
  19.3 0.7 copy-start.2
  24.7 40.2 %copy-start.1 = (s32[1,18]{1,0:T(1,128)S(1)}, s32[1,18]{1,0:T(1,128)}, u32[]{:S(2)}) copy-start(s32[1,18]{1,0:T(1,128)} %param.16) | copy-start | bytes 220
  49.3 15.5 %all-to-all-start.2 = ((bf16[32,8,512]{2,1,0:T(8,128)(2,1)}), bf16[32,8,512]{2,1,0:T(8,128)(2,1)S(1)}, u32[]{:S(2)}, u32[]{:S(2)}) async-start(bf16[32,8,512]{2,1,0:T(8,128)(2,1)} %get-tuple-element.50), calls=%async_computation.2 | async-start | bytes 524288 | tf_op jit(solution)/shard_map/all_to_all | solution.py:296
  53.4 4.7 %collective-permute-start.3 = (f32[8,512]{1,0:T(8,128)S(1)}, f32[8,512]{1,0:T(8,128)S(1)}, u32[]{:S(2)}, u32[]{:S(2)}) collective-permute-start(f32[8,512]{1,0:T(8,128)S(1)} %get-tuple-element.51.refs_1_), channel_id=1, source_target_pairs={{1,0},{2,1},{3,2},{4,3},{5,4},{6,5},{7,6},{8,7},{9,8},{10,9},{11,1... | collective-permute-start | bytes 49160 | tf_op jit(solution)/shard_map/ppermute | solution.py:302
  53.5 4.7 %collective-permute-start.2 = (f32[8,512]{1,0:T(8,128)S(1)}, f32[8,512]{1,0:T(8,128)S(1)}, u32[]{:S(2)}, u32[]{:S(2)}) collective-permute-start(f32[8,512]{1,0:T(8,128)S(1)} %get-tuple-element.51.refs_1_), channel_id=1, source_target_pairs={{0,1},{1,2},{2,3},{3,4},{4,5},{5,6},{6,7},{7,8},{8,9},{9,10},{10,1... | collective-permute-start | bytes 49160 | tf_op jit(solution)/shard_map/ppermute | solution.py:301

commit v4 on v3

--- a/solution.py
+++ b/solution.py
@@ -77,10 +77,10 @@
     return pl.multiple_of(jnp.minimum((offset >> 4) << 4, N - WINDOW), ALIGN)
 
 
-def taps_kernel(count_ref, row_off, col_off, *refs):
-    sources, (wx_hbm, wy_hbm, wx_keep, wy_keep), kept, held = refs[:7], refs[7:11], refs[11:14], refs[14:18]
-    wx_ref, wy_ref, in_sems, out_sems = refs[18:]
-    row_first, col_first, row_taps, col_taps = held
+def taps_kernel(count_ref, *refs):
+    sources, (wx_hbm, wy_hbm, wx_keep, wy_keep), kept, held = refs[:9], refs[9:13], refs[13:16], refs[16:22]
+    wx_ref, wy_ref, in_sems, out_sems = refs[22:]
+    row_off, col_off, row_first, col_first, row_taps, col_taps = held
     loads = [pltpu.make_async_copy(source, own, in_sems.at[k]) for k, (source, own) in enumerate(zip(sources, held + kept))]
     for load in loads:
         load.start()
@@ -103,8 +103,8 @@
         return values.astype(bf16)
 
     def build(block, wx_out, wy_out, place):
-        col = col_off[block]
-        wx_out[place] = matrix(N, row_first[block] + row_off[block], row_taps[0, block].astype(f32))
+        col = col_off[0, block]
+        wx_out[place] = matrix(N, row_first[block] + row_off[0, block], row_taps[0, block].astype(f32))
         wy_out[place] = matrix(WINDOW, col_first[block] + (col - window_start(col)), col_taps[0, block].astype(f32))
 
     def first(block, carry):
@@ -140,12 +140,12 @@
 
 
 def coil_kernel(last, *refs):
-    (count_ref, col_off, image_ref, maps_ref, samples_ref, fwd_ref, wx_keep, wy_keep, wx_hbm, wy_hbm) = refs[:10]
+    (count_ref, image_ref, maps_ref, samples_ref, fwd_ref, wx_keep, wy_keep, wx_hbm, wy_hbm, col_off_hbm) = refs[:10]
     if last:
         (before_ref, send_ref) = refs[10:12]
     else:
         (send_ref, misfit_ref) = refs[10:12]
-    (wx_ref, wy_ref, kspace_ref, grid_ref, sems) = refs[12:]
+    (col_off, wx_ref, wy_ref, kspace_ref, grid_ref, sems, off_sem) = refs[12:]
     count = count_ref[0]
     groups = (count + GROUP - 1) // GROUP
 
@@ -161,6 +161,8 @@
             copy.start()
         return carry
 
+    off_copy = pltpu.make_async_copy(col_off_hbm, col_off, off_sem)
+    off_copy.start()
     lax.fori_loop(1, groups, fetch, 0)
 
     image = image_ref[...].astype(f32)
@@ -181,7 +183,7 @@
         for member in range(GROUP):
             block = group * GROUP + member
             place = member if wx_in is wx_keep else block - GROUP
-            window = pl.ds(window_start(col_off[block]), WINDOW)
+            window = pl.ds(window_start(col_off[0, block]), WINDOW)
             wx = wx_in[place]
             wy = wy_in[place]
             wy_wide = wy.astype(f32)
@@ -204,6 +206,7 @@
             copy.wait()
         return visit(group, wx_ref, wy_ref, misfit)
 
+    off_copy.wait()
     misfit = visit(0, wx_keep, wy_keep, jnp.zeros((1, BS), f32))
     misfit = lax.fori_loop(1, groups, later, misfit)
     misfit = jnp.broadcast_to(jnp.sum(misfit, axis=1, keepdims=True), (8, 128))
@@ -338,8 +341,6 @@
     firsts = (NB, 1, BS)
     wx_shape = (NB - GROUP, N, BS)
     wy_shape = (NB - GROUP, WINDOW, BS)
-    row_off = row_offset.reshape(NB)
-    col_off = col_offset.reshape(NB)
     constants = pl.pallas_call(
         taps_kernel,
         out_shape=(
@@ -351,25 +352,25 @@
             pltpu.VMEM(coil_maps.shape, bf16),
             pltpu.VMEM(samples.shape, bf16),
         ),
-        in_specs=[smem(), smem(), smem()] + [hbm() for _ in range(7)],
+        in_specs=[smem()] + [hbm() for _ in range(9)],
         out_specs=(hbm(), hbm(), vmem(), vmem(), vmem(), vmem(), vmem()),
         scratch_shapes=[
+            pltpu.SMEM(row_offset.shape, jnp.int32),
+            pltpu.SMEM(col_offset.shape, jnp.int32),
             pltpu.VMEM(firsts, jnp.int32),
             pltpu.VMEM(firsts, jnp.int32),
             pltpu.VMEM(row_taps.shape, bf16),
             pltpu.VMEM(col_taps.shape, bf16),
             pltpu.VMEM(wx_shape, bf16),
             pltpu.VMEM(wy_shape, bf16),
-            pltpu.SemaphoreType.DMA((7,)),
+            pltpu.SemaphoreType.DMA((9,)),
             pltpu.SemaphoreType.DMA((2, NG)),
         ],
         compiler_params=params,
         name="taps",
     )(
         blocks_used,
-        row_off,
-        col_off,
-        *map(in_hbm, (row_first.reshape(firsts), col_first.reshape(firsts), row_taps, col_taps)),
+        *map(in_hbm, (row_offset, col_offset, row_first.reshape(firsts), col_first.reshape(firsts), row_taps, col_taps)),
         *map(in_hbm, (forward, coil_maps, samples)),
     )
 
@@ -384,8 +385,8 @@
             wx, wy, wx_keep, wy_keep, forward, maps, measured = constants
         else:
             gathered, left, right = lax.optimization_barrier((gathered, left, right))
-        inputs = [blocks_used, col_off, gathered, maps, measured, forward, wx_keep, wy_keep, in_hbm(wx), in_hbm(wy)]
-        specs = [smem(), smem()] + [vmem() for _ in range(6)] + [hbm(), hbm()]
+        inputs = [blocks_used, gathered, maps, measured, forward, wx_keep, wy_keep, *map(in_hbm, (wx, wy, col_offset))]
+        specs = [smem()] + [vmem() for _ in range(6)] + [hbm() for _ in range(3)]
         if last:
             inputs.append(misfit)
             specs.append(vmem())
@@ -398,11 +399,13 @@
             in_specs=specs,
             out_specs=tuple(vmem() for _ in out_shape),
             scratch_shapes=[
+                pltpu.SMEM(col_offset.shape, jnp.int32),
                 pltpu.VMEM(wx_shape, bf16),
                 pltpu.VMEM(wy_shape, bf16),
                 pltpu.VMEM((2, N, N), bf16),
                 pltpu.VMEM((2, N, N), f32),
                 pltpu.SemaphoreType.DMA((2, NG)),
+                pltpu.SemaphoreType.DMA,
             ],
             compiler_params=params,
             name=f"coil{step_num}",

time: 88.8 us -> 86 us (0.968)
  the two profiles are of different devices: /device:TPU:57 before, /device:TPU:40 now
where the time goes in v4:
time: 86 us; the launch traced here: 85.2 us
  blocking collectives  34.1 us (40%)
  waiting for transfers between devices  19.7 us (23%)
  starting transfers between devices  18.6 us (22%)
  Pallas kernels  11.5 us (13%)
  between operations  1.36 us (2%)
    all_to_all x2, blocking collectives, exchanged(): return lax.all_to_all(parts, 'coil', 0, 0, tiled=True)  34.1 us
    all_to_all x2, starting transfers between devices, exchanged(): return lax.all_to_all(parts, 'coil', 0, 0, tiled=True)  17.6 us
    all_to_all x2, waiting for transfers between devices, exchanged(): return lax.all_to_all(parts, 'coil', 0, 0, tiled=True)  17 us
    pallas_call x2, Pallas kernels, on_device(): pl.pallas_call(lambda *refs, last=last: coil_kernel(last, *refs), out_sha...  5.74 us
    pallas_call x1, Pallas kernels, on_device(): pl.pallas_call(taps_kernel, out_shape=(pltpu.HBM(wx_shape, bf16), pltpu.H...  2.6 us
    ppermute x2, waiting for transfers between devices, neighbours(): lax.ppermute(values, 'frame', [(i, (i + 1) % count) for i in range(count)])  1.74 us
  transfers between devices with their start and end apart: 6, of which 4 were waited for; matrix products, arithmetic and copies ran while one was open for 0% of the time, Pallas kernels for 3%

profile of v4, /device:TPU:40, one launch (start us, length us, event | category | flops | bytes accessed | tf_op | source)
XLA Modules:
  0.0 85.2 jit_solution(13925788437873171156)
XLA Ops:
  0.6 1.5 %start.1 = (bf16[32,8,512]{2,1,0:T(8,128)(2,1)}, f32[8,512]{1,0:T(8,128)S(1)}) custom-call(f32[8,1,2,256]{3,2,1,0:T(2,128)} %image_hbm.1), custom_call_target="tpu_custom_call" | custom-call | tf_op jit(solution)/shard_map/start/pallas_call | solution.py:330
  2.1 13.2 %all-to-all-start = ((bf16[32,8,512]{2,1,0:T(8,128)(2,1)}), bf16[32,8,512]{2,1,0:T(8,128)(2,1)S(1)}, u32[]{:S(2)}, u32[]{:S(2)}) async-start(bf16[32,8,512]{2,1,0:T(8,128)(2,1)} %get-tuple-element.30), calls=%async_computation | async-start | bytes 524288 | tf_op jit(solution)/shard_map/all_to_all | solution.py:299
  15.3 0.5 collective-permute-start.1
  15.8 0.0 collective-permute-start
  16.5 2.6 %taps.1 = (bf16[12,256,256]{2,1,0:T(8,128)(2,1)}, bf16[12,144,256]{2,1,0:T(8,128)(2,1)}, bf16[6,256,256]{2,1,0:T(8,128)(2,1)S(1)}, bf16[6,144,256]{2,1,0:T(8,128...) custom-call(s32[1]{0:T(128)S(6)} %copy.13.count_ref.refs_0_, ...), custom_call_target="tpu_custom_call" | custom-call | tf_op jit(solution)/shard_map/taps/pallas_call | solution.py:344
  19.1 0.0 collective-permute-done.1.refs_3_
  19.1 0.0 collective-permute-done.refs_2_
  19.1 8.6 %all-to-all-done.refs_1_ = bf16[32,8,512]{2,1,0:T(8,128)(2,1)S(1)} async-done(((bf16[32,8,512]{2,1,0:T(8,128)(2,1)}), bf16[32,8,512]{2,1,0:T(8,128)(2,1)S(1)}, u32[]{:S(2)}, u32[]{:S(2)}) %all-to-all-start) | async-done | bytes 262176 | tf_op jit(solution)/shard_map/all_to_all | solution.py:299
  27.7 2.9 %coil0.1 = (bf16[32,8,512]{2,1,0:T(8,128)(2,1)S(1)}, f32[8,128]{1,0:T(8,128)S(1)}) custom-call(s32[1]{0:T(128)S(6)} %copy.13.count_ref.refs_0_, bf16[32,8,512]{2,1,0:T(8,128)(2,1)S(1)} %all-to-all-done.refs_1_, bf16[1,2,256,256]{3,2,1,0:T(8,128)(2,1)S(1)} %get-tuple-element.40.refs_2_, bf16[1,1,18,2,256]{4,3,2,1,0:T(2,128)(2,1)S(1)} %get-tuple-element.41.refs_3_, ...), custom_call_target="tpu_custom_call" | custom-call | tf_op jit(solution)/shard_map/coil0/pallas_call | solution.py:396
  30.6 16.6 %all_to_all.20.refs_0_ = bf16[32,8,512]{2,1,0:T(8,128)(2,1)S(1)} all-to-all(bf16[32,8,512]{2,1,0:T(8,128)(2,1)S(1)} %get-tuple-element.47), channel_id=1, replica_groups=mesh['coil'=32,'frame'=16] {'coil'}, dimensions={0} | all-to-all | bytes 524288 | tf_op jit(solution)/shard_map/all_to_all | solution.py:299
  47.2 0.9 %update0.1 = (bf16[32,8,512]{2,1,0:T(8,128)(2,1)}, f32[8,512]{1,0:T(8,128)S(1)}) custom-call(bf16[32,8,512]{2,1,0:T(8,128)(2,1)S(1)} %all_to_all.20.refs_0_, f32[8,512]{1,0:T(8,128)S(1)} %get-tuple-element.31.refs_1_.refs_4_, f32[8,512]{1,0:T(8,128)S(1)} %collective-permute-done.refs_2_, f32[8,512]{1,0:T(8,128)S(1)} %collective-permute-done.1.refs_3_, ...), custom_call_target="tpu_custom_call" | custom-call | tf_op jit(solution)/shard_map/update0/pallas_call | solution.py:425
  48.2 4.4 %all-to-all-start.2 = ((bf16[32,8,512]{2,1,0:T(8,128)(2,1)}), bf16[32,8,512]{2,1,0:T(8,128)(2,1)S(1)}, u32[]{:S(2)}, u32[]{:S(2)}) async-start(bf16[32,8,512]{2,1,0:T(8,128)(2,1)} %get-tuple-element.50), calls=%async_computation.2 | async-start | bytes 524288 | tf_op jit(solution)/shard_map/all_to_all | solution.py:299
  52.6 0.0 collective-permute-start.3
  52.6 0.5 collective-permute-start.2
  53.1 0.9 %collective-permute-done.3.refs_3_ = f32[8,512]{1,0:T(8,128)S(1)} collective-permute-done((f32[8,512]{1,0:T(8,128)S(1)}, f32[8,512]{1,0:T(8,128)S(1)}, u32[]{:S(2)}, u32[]{:S(2)}) %collective-permute-start.3) | collective-permute-done | bytes 16416 | tf_op jit(solution)/shard_map/ppermute | solution.py:305
  54.0 1.7 %collective-permute-done.2.refs_2_ = f32[8,512]{1,0:T(8,128)S(1)} collective-permute-done((f32[8,512]{1,0:T(8,128)S(1)}, f32[8,512]{1,0:T(8,128)S(1)}, u32[]{:S(2)}, u32[]{:S(2)}) %collective-permute-start.2) | collective-permute-done | bytes 16416 | tf_op jit(solution)/shard_map/ppermute | solution.py:304
  55.8 8.4 %all-to-all-done.2.refs_1_ = bf16[32,8,512]{2,1,0:T(8,128)(2,1)S(1)} async-done(((bf16[32,8,512]{2,1,0:T(8,128)(2,1)}), bf16[32,8,512]{2,1,0:T(8,128)(2,1)S(1)}, u32[]{:S(2)}, u32[]{:S(2)}) %all-to-all-start.2) | async-done | bytes 262176 | tf_op jit(solution)/shard_map/all_to_all | solution.py:299
  64.1 2.9 %coil1.1 = bf16[32,8,640]{2,1,0:T(8,128)(2,1)S(1)} custom-call(s32[1]{0:T(128)S(6)} %copy.13.count_ref.refs_0_, bf16[32,8,512]{2,1,0:T(8,128)(2,1)S(1)} %all-to-all-done.2.refs_1_, bf16[1,2,256,256]{3,2,1,0:T(8,128)(2,1)S(1)} %get-tuple-element.40.refs_2_, bf16[1,1,18,2,256]{4,3,2,1,0:T(2,128)(2,1)S(1)} %get-tuple-element.41.refs_3_, ...), custom_call_target="tpu_custom_call" | custom-call | tf_op jit(solution)/shard_map/coil1/pallas_call | solution.py:396
  67.0 17.4 %all_to_all.21.refs_0_ = bf16[32,8,640]{2,1,0:T(8,128)(2,1)S(1)} all-to-all(bf16[32,8,640]{2,1,0:T(8,128)(2,1)S(1)} %coil1.1), channel_id=1, replica_groups=mesh['coil'=32,'frame'=16] {'coil'}, dimensions={0} | all-to-all | bytes 655360 | tf_op jit(solution)/shard_map/all_to_all | solution.py:299
  84.5 0.8 update1.1
Async XLA Ops:
  2.1 25.6 %all-to-all-start = ((bf16[32,8,512]{2,1,0:T(8,128)(2,1)}), bf16[32,8,512]{2,1,0:T(8,128)(2,1)S(1)}, u32[]{:S(2)}, u32[]{:S(2)}) async-start(bf16[32,8,512]{2,1,0:T(8,128)(2,1)} %get-tuple-element.30), calls=%async_computation | async-start | bytes 524288 | tf_op jit(solution)/shard_map/all_to_all | solution.py:299
  15.3 3.8 %collective-permute-start.1 = (f32[8,512]{1,0:T(8,128)S(1)}, f32[8,512]{1,0:T(8,128)S(1)}, u32[]{:S(2)}, u32[]{:S(2)}) collective-permute-start(f32[8,512]{1,0:T(8,128)S(1)} %get-tuple-element.31.refs_1_.refs_4_), channel_id=1, source_target_pairs={{1,0},{2,1},{3,2},{4,3},{5,4},{6,5},{7,6},{8,7},{9,8},{10,9},{11,1... | collective-permute-start | bytes 49160 | tf_op jit(solution)/shard_map/ppermute | solution.py:305
  15.8 3.3 %collective-permute-start = (f32[8,512]{1,0:T(8,128)S(1)}, f32[8,512]{1,0:T(8,128)S(1)}, u32[]{:S(2)}, u32[]{:S(2)}) collective-permute-start(f32[8,512]{1,0:T(8,128)S(1)} %get-tuple-element.31.refs_1_.refs_4_), channel_id=1, source_target_pairs={{0,1},{1,2},{2,3},{3,4},{4,5},{5,6},{6,7},{7,8},{8,9},{9,10},{10,1... | collective-permute-start | bytes 49160 | tf_op jit(solution)/shard_map/ppermute | solution.py:304
  48.2 16.0 %all-to-all-start.2 = ((bf16[32,8,512]{2,1,0:T(8,128)(2,1)}), bf16[32,8,512]{2,1,0:T(8,128)(2,1)S(1)}, u32[]{:S(2)}, u32[]{:S(2)}) async-start(bf16[32,8,512]{2,1,0:T(8,128)(2,1)} %get-tuple-element.50), calls=%async_computation.2 | async-start | bytes 524288 | tf_op jit(solution)/shard_map/all_to_all | solution.py:299
  52.6 1.5 %collective-permute-start.3 = (f32[8,512]{1,0:T(8,128)S(1)}, f32[8,512]{1,0:T(8,128)S(1)}, u32[]{:S(2)}, u32[]{:S(2)}) collective-permute-start(f32[8,512]{1,0:T(8,128)S(1)} %get-tuple-element.51.refs_1_), channel_id=1, source_target_pairs={{1,0},{2,1},{3,2},{4,3},{5,4},{6,5},{7,6},{8,7},{9,8},{10,9},{11,1... | collective-permute-start | bytes 49160 | tf_op jit(solution)/shard_map/ppermute | solution.py:305
  52.6 3.2 %collective-permute-start.2 = (f32[8,512]{1,0:T(8,128)S(1)}, f32[8,512]{1,0:T(8,128)S(1)}, u32[]{:S(2)}, u32[]{:S(2)}) collective-permute-start(f32[8,512]{1,0:T(8,128)S(1)} %get-tuple-element.51.refs_1_), channel_id=1, source_target_pairs={{0,1},{1,2},{2,3},{3,4},{4,5},{5,6},{6,7},{7,8},{8,9},{9,10},{10,1... | collective-permute-start | bytes 49160 | tf_op jit(solution)/shard_map/ppermute | solution.py:304
